TPU v7x, 32 devices: a 4x4x1 block of a 4x4x8 slice. The times are simulated.
32 devices in a mesh: dp: 1 (over z), tp: 4 (over y), sp: 8 (over x, core).
Axes of the slice: x: 4, y: 4, z: 1, core: 2. Of those that a mesh axis runs over, the one named last changes fastest.
The devices are a block of a 4x4x8 slice.
Arguments:
- x_tokens: bfloat16 [2048, 8192], P(('dp', 'sp'), 'tp')
- doc_ids: int32 [2048], P(('dp', 'sp'))
- w_qkv: bfloat16 [8192, 24576], P('sp', 'tp')
- w_out: bfloat16 [8192, 8192], P('sp', 'tp')
Outputs:
- output: bfloat16 [2048, 8192], P(('dp', 'sp', 'tp'))
All inputs are finite; a program needn't handle non-finite values.
Results may differ from a plain program's by a relative error of at most 0.00311.
Values are sent between devices in bfloat16 or wider.
A program may use at most 768 MiB of HBM per device.

v0:
```python
import jax
import jax.numpy as jnp
from jax import lax
from jax.sharding import PartitionSpec as P

HEAD_DIM = 128
SOFTMAX_SCALE = HEAD_DIM ** -0.5


def solution(mesh):
    def device_block(x_block, doc_block, wqkv_block, wout_block):
        x_rows = lax.all_gather(x_block, "tp", axis=1, tiled=True)
        wqkv_cols = lax.all_gather(wqkv_block, "sp", axis=0, tiled=True)
        qkv_local = jnp.dot(x_rows, wqkv_cols, preferred_element_type=jnp.float32).astype(jnp.bfloat16)
        row_count = x_rows.shape[0]
        head_count = wqkv_cols.shape[1] // (3 * HEAD_DIM)
        qkv_local = qkv_local.reshape(row_count, head_count, 3, HEAD_DIM)
        query_loc = qkv_local[:, :, 0]
        kv_all = lax.all_gather(qkv_local[:, :, 1:], "sp", axis=0, tiled=True)
        doc_all = lax.all_gather(doc_block, "sp", axis=0, tiled=True)
        scores = jnp.einsum("qhd,khd->hqk", query_loc, kv_all[:, :, 0], preferred_element_type=jnp.float32) * SOFTMAX_SCALE
        same_doc = doc_block[:, None] == doc_all[None, :]
        scores = jnp.where(same_doc[None], scores, -jnp.inf)
        weights = jax.nn.softmax(scores, axis=-1).astype(jnp.bfloat16)
        context = jnp.einsum("hqk,khd->qhd", weights, kv_all[:, :, 1], preferred_element_type=jnp.float32).astype(jnp.bfloat16)
        context = context.reshape(row_count, head_count * HEAD_DIM)
        ctx_rows = lax.all_gather(context, "tp", axis=1, tiled=True)
        wout_cols = lax.all_gather(wout_block, "sp", axis=0, tiled=True)
        y_block = jnp.dot(ctx_rows, wout_cols, preferred_element_type=jnp.float32).astype(jnp.bfloat16)
        return lax.all_to_all(y_block, "tp", 0, 1, tiled=True)

    return jax.shard_map(
        device_block,
        mesh=mesh,
        in_specs=(P(("dp", "sp"), "tp"), P(("dp", "sp")), P("sp", "tp"), P("sp", "tp")),
        out_specs=P(("dp", "sp", "tp"), None),
        check_vma=False,
    )
```

profile of v0, /device:TPU:98, one launch (start us, length us, event | category | flops | bytes accessed | tf_op | source)
XLA Modules:
  0.0 872.0 jit_solution(13382825657141733665)
XLA Ops:
  6.5 0.0 all-gather.7.cloned.1.call-start
  6.6 0.7 all-gather.7.cloned.1.call-update
  7.3 0.1 all-gather.9.cloned.1.call-start
  7.4 0.7 all-gather.9.cloned.1.call-update
  8.1 0.1 all-gather.11.cloned.1.call-start
  8.2 49.3 %all-gather.7.cloned.1.call-done = bf16[256,8192]{1,0:T(8,128)(2,1)} async-done(((bf16[256,2048]{1,0:T(8,128)(2,1)}), bf16[256,8192]{1,0:T(8,128)(2,1)}) %all-gather.7.cloned.1.call-update) | async-done | bytes 4194320 | tf_op jit(solution)/shard_map/all_gather | solution.py:12
  57.5 436.4 %all-gather.9.cloned.1.call-done = bf16[8192,6144]{1,0:T(8,128)(2,1)} async-done(((bf16[1024,6144]{1,0:T(8,128)(2,1)}), bf16[8192,6144]{1,0:T(8,128)(2,1)}) %all-gather.9.cloned.1.call-update) | async-done | bytes 100663312 | tf_op jit(solution)/shard_map/all_gather | solution.py:13
  493.9 39.6 %convolution_convert_fusion = bf16[256,6144]{1,0:T(8,128)(2,1)} fusion(bf16[256,8192]{1,0:T(8,128)(2,1)} %all-gather.7.cloned.1.call-done, bf16[8192,6144]{1,0:T(8,128)(2,1)} %all-gather.9.cloned.1.call-done), kind=kOutput, calls=%fused_computation.12 | convolution fusion | flops 25771376640 | bytes 108003328 | tf_op jit(solution)/shard_map/dot_general | solution.py:14
  533.5 0.0 copy-start
  533.5 3.2 copy.14
  536.6 1.5 slice.16
  538.1 3.9 copy.20
  542.0 0.1 all-gather.11.cloned.1.call-update
  542.1 0.1 all-gather.15.cloned.1.call-start
  542.2 0.6 all-gather.15.cloned.1.call-update
  542.7 0.1 all-gather.13.cloned.1.call-start
  542.8 0.0 copy-done
  542.8 22.2 %all-gather = s32[8,1,256]{2,1,0:T(1,128)S(1)} all-gather(s32[1,1,256]{2,1,0:T(1,128)S(1)} %bitcast.32), channel_id=1, replica_groups=mesh['dp'=1,'tp'=4,'sp'=8] {'sp'}, dimensions={0}, use_global_device_ids=true | all-gather | bytes 9216 | tf_op jit(solution)/shard_map/all_gather | solution.py:20
  565.1 1.2 broadcast_compare_fusion
  566.2 59.2 %all-gather.11.cloned.1.call-done = bf16[2048,16,2,128]{3,0,1,2:T(8,128)(2,1)} async-done(((bf16[256,16,2,128]{3,0,1,2:T(8,128)(2,1)}), bf16[2048,16,2,128]{3,0,1,2:T(8,128)(2,1)}) %all-gather.11.cloned.1.call-update) | async-done | bytes 16777232 | tf_op jit(solution)/shard_map/all_gather | solution.py:19
  625.5 16.5 %fusion.6 = f32[16,256,2048]{2,1,0:T(8,128)} fusion(bf16[2048,16,2,128]{3,0,1,2:T(8,128)(2,1)} %all-gather.11.cloned.1.call-done, bf16[256,16,3,128]{0,3,2,1:T(8,128)(2,1)S(1)} %bitcast.27), kind=kOutput, calls=%fused_computation.10 | convolution fusion | flops 2147483648 | bytes 42991616 | tf_op jit(solution)/shard_map/qhd,khd->hqk/dot_general | solution.py:21
  641.9 38.0 %fusion.10 = (f32[16,256]{1,0:T(8,128)S(1)}, f32[16,256,2048]{2,1,0:T(8,128)}) fusion(f32[16,256,2048]{2,1,0:T(8,128)} %fusion.6, pred[256,2048]{1,0:T(8,128)(4,1)} %broadcast_compare_fusion), kind=kOutput, calls=%fused_computation.19 | output fusion | flops 50333696 | bytes 67649536 | tf_op jit(solution)/shard_map/sub | solution.py:24
  680.0 16.1 %fusion.7 = bf16[16,128,256]{2,1,0:T(8,128)(2,1)} fusion(f32[16,256,2048]{2,1,0:T(8,128)} %get-tuple-element.6, f32[16,256]{1,0:T(8,128)S(1)} %get-tuple-element.5, bf16[2048,16,2,128]{3,0,1,2:T(8,128)(2,1)} %all-gather.11.cloned.1.call-done), kind=kOutput, calls=%fused_computation.14 | convolution fusion | flops 2164785152 | bytes 43008000 | tf_op jit(solution)/shard_map/hqk,khd->qhd/dot_general | solution.py:25
  696.1 0.1 all-gather.13.cloned.1.call-update
  696.1 86.0 %all-gather.15.cloned.1.call-done = bf16[8192,2048]{1,0:T(8,128)(2,1)} async-done(((bf16[1024,2048]{1,0:T(8,128)(2,1)}), bf16[8192,2048]{1,0:T(8,128)(2,1)}) %all-gather.15.cloned.1.call-update) | async-done | bytes 33554448 | tf_op jit(solution)/shard_map/all_gather | solution.py:28
  782.1 47.9 %all-gather.13.cloned.1.call-done = bf16[256,8192]{0,1:T(8,128)(2,1)} async-done(((bf16[256,2048]{0,1:T(8,128)(2,1)}), bf16[256,8192]{0,1:T(8,128)(2,1)}) %all-gather.13.cloned.1.call-update) | async-done | bytes 4194320 | tf_op jit(solution)/shard_map/all_gather | solution.py:27
  830.0 16.3 %convolution_convert_fusion.1 = bf16[256,2048]{1,0:T(8,128)(2,1)S(1)} fusion(bf16[256,8192]{0,1:T(8,128)(2,1)} %all-gather.13.cloned.1.call-done, bf16[8192,2048]{1,0:T(8,128)(2,1)} %all-gather.15.cloned.1.call-done), kind=kOutput, calls=%fused_computation.13 | convolution fusion | flops 8590458880 | bytes 38797312 | tf_op jit(solution)/shard_map/dot_general | solution.py:29
  846.3 18.1 %all_to_all.19 = bf16[4,64,2048]{2,1,0:T(8,128)(2,1)S(1)} all-to-all(bf16[4,64,2048]{2,1,0:T(8,128)(2,1)S(1)} %bitcast.28), channel_id=1, replica_groups=mesh['dp'=1,'tp'=4,'sp'=8] {'tp'}, dimensions={0} | all-to-all | bytes 2097152 | tf_op jit(solution)/shard_map/all_to_all | solution.py:30
  864.4 1.0 copy.22
Async XLA Ops:
  6.5 51.0 %all-gather.7.cloned.1.call-start = ((), (), s32[]{:S(2)}) async-start(), calls=%async_computation.1 | async-start | bytes 5242880 | tf_op jit(solution)/shard_map/all_gather | solution.py:12
  7.3 486.6 %all-gather.9.cloned.1.call-start = ((), (), s32[]{:S(2)}) async-start(), calls=%async_computation.2 | async-start | bytes 113246208 | tf_op jit(solution)/shard_map/all_gather | solution.py:13
  8.1 617.3 %all-gather.11.cloned.1.call-start = ((), (), s32[]{:S(2)}) async-start(), calls=%async_computation.3 | async-start | bytes 18874368 | tf_op jit(solution)/shard_map/all_gather | solution.py:19
  533.5 9.3 %copy-start = (s32[256]{0:T(256)S(1)}, s32[256]{0:T(256)}, u32[]{:S(2)}) copy-start(s32[256]{0:T(256)} %param.5) | copy-start | bytes 3076
  542.1 240.0 %all-gather.15.cloned.1.call-start = ((), (), s32[]{:S(2)}) async-start(), calls=%async_computation.5 | async-start | bytes 37748736 | tf_op jit(solution)/shard_map/all_gather | solution.py:28
  542.7 287.3 %all-gather.13.cloned.1.call-start = ((), (), s32[]{:S(2)}) async-start(), calls=%async_computation.4 | async-start | bytes 5242880 | tf_op jit(solution)/shard_map/all_gather | solution.py:27
Sparse Core Ops, SparseCore 0:
  8.9 48.5 all-gather.6
  59.1 434.7 all-gather.8
  542.2 83.2 all-gather.10
  626.9 155.1 all-gather.14
  783.5 46.4 all-gather.12
where the time goes:
time: 872 us
  waiting for transfers between devices  681 us (78%)
  matrix products  88.4 us (10%)
  blocking collectives  40.3 us (5%)
  other arithmetic  39.2 us (4%)
  between operations  13.2 us (2%)
  local copies, waits for them, and re-layouts  9.6 us (1%)
    all_gather x1, waiting for transfers between devices, device_block(): wqkv_cols = lax.all_gather(wqkv_block, 'sp', axis=0, tiled=True)  436 us
    all_gather x1, waiting for transfers between devices, device_block(): wout_cols = lax.all_gather(wout_block, 'sp', axis=0, tiled=True)  86 us
    all_gather x1, waiting for transfers between devices, device_block(): kv_all = lax.all_gather(qkv_local[:, :, 1:], 'sp', axis=0, tiled=True)  59.2 us
    all_gather x1, waiting for transfers between devices, device_block(): x_rows = lax.all_gather(x_block, 'tp', axis=1, tiled=True)  49.3 us
    all_gather x1, waiting for transfers between devices, device_block(): ctx_rows = lax.all_gather(context, 'tp', axis=1, tiled=True)  47.9 us
    dot_general x1, matrix products, device_block(): jnp.dot(x_rows, wqkv_cols, preferred_element_type=jnp.float32)  39.6 us
    sub x1, other arithmetic, device_block(): weights = jax.nn.softmax(scores, axis=-1).astype(jnp.bfloat16)  38 us
    all_gather x1, blocking collectives, device_block(): doc_all = lax.all_gather(doc_block, 'sp', axis=0, tiled=True)  22.2 us
  transfers between devices with their start and end apart: 5, of which 5 were waited for; matrix products, arithmetic and copies ran while one was open for 8% of the time, Pallas kernels for 0%

commit v1 on v0

v1 whole, which is shorter than its diff:
```python
import functools

import jax
import jax.numpy as jnp
from jax import lax
from jax.experimental import pallas as pl
from jax.experimental.pallas import tpu as pltpu
from jax.sharding import PartitionSpec as P

HEAD_DIM = 128
SOFTMAX_SCALE = HEAD_DIM ** -0.5
MESH = pl.DeviceIdType.MESH
HW = 3 * HEAD_DIM
BF16 = jnp.bfloat16
F32 = jnp.float32
ANY = pl.BlockSpec(memory_space=pl.ANY)
VM = pl.BlockSpec(memory_space=pltpu.VMEM)
ROWS_MM = 256


def _place(nsp, ntp):
    sp, y = lax.axis_index("sp"), lax.axis_index("tp")
    x, c = sp // 2, sp % 2
    nx = nsp // 2
    xs = [x, lax.rem(x + nx - 1, nx), lax.rem(x + 1, nx), lax.rem(x + 2, nx)]
    ys = [y, lax.rem(y + ntp - 1, ntp), lax.rem(y + 1, ntp), lax.rem(y + 2, ntp)]
    return sp, y, c, xs, ys


def qkv_kernel(nsp, ntp, x_ref, seg_ref, w_ref, qkv_ref, xall, wall, wst, segall,
               acc, xbuf, wbuf, xown, sown, loc, xs_s, xs_r, y_s, y_r, p_s, p_r, w_s, w_r, s_s, s_r):
    sp, y, c, xs, ys = _place(nsp, ntp)
    rows, kcols = x_ref.shape
    krows = w_ref.shape[0]
    half, khalf = rows // 2, krows // 2
    tokens = rows * nsp

    def dev(xi, ci, yi):
        return {"sp": 2 * xi + ci, "tp": yi}

    def rc(src, dst, ss, rs, to):
        return pltpu.make_async_remote_copy(
            src_ref=src, dst_ref=dst, send_sem=ss, recv_sem=rs, device_id=to, device_id_type=MESH)

    own_in = pltpu.make_async_copy(x_ref, xown, loc.at[0])
    own_in.start()

    barrier = pltpu.get_barrier_semaphore()
    greet = []
    for i in (1, 2, 3):
        for ci in (0, 1):
            greet.append(dev(xs[i], ci, y))
    greet.append(dev(xs[0], 1 - c, y))
    greet += [dev(xs[0], c, ys[1]), dev(xs[0], c, ys[2])]
    for d in greet:
        pl.semaphore_signal(barrier, inc=1, device_id=d, device_id_type=MESH)
    pl.semaphore_wait(barrier, len(greet))

    sends = []

    def go(cp):
        cp.start()
        sends.append(cp)

    partner = dev(xs[0], 1 - c, y)
    left, right = (xs[1], c, y), (xs[2], c, y)

    def blk(yi, xi):
        return xall.at[yi, 2 * xi + c]

    go(rc(x_ref, blk(y, xs[0]), xs_s.at[0], xs_r.at[0], dev(*right)))
    go(rc(x_ref, blk(y, xs[0]), xs_s.at[1], xs_r.at[1], dev(*left)))
    go(rc(x_ref, blk(y, xs[0]), y_s.at[0, 0], y_r.at[0, 0], dev(xs[0], c, ys[2])))
    go(rc(x_ref, blk(y, xs[0]), y_s.at[1, 0], y_r.at[1, 0], dev(xs[0], c, ys[1])))
    go(rc(x_ref, blk(y, xs[0]), p_s.at[0, 0], p_r.at[0, 0], partner))
    n = 0
    for i in range(4):
        for ci in (0, 1):
            if i == 0 and ci == 1:
                continue
            cc = (1 - c) if i == 0 else ci
            back = {0: 0, 1: 2, 2: 1, 3: 3}[i]
            go(rc(seg_ref, segall.at[sp], s_s.at[n], s_r.at[back, c], dev(xs[i], cc, y)))
            n += 1

    def wcol(h, j, num):
        return pl.ds(pl.multiple_of((h * nsp + j) * HW, 128), num * HW)

    def w_far(h):
        go(rc(w_ref.at[pl.ds(0, khalf), wcol(h, 2 * xs[3], 2)], wst.at[0, h], w_s.at[h, 0], w_r.at[h, 0], dev(*right)))
        go(rc(w_ref.at[pl.ds(khalf, khalf), wcol(h, 2 * xs[3], 2)], wst.at[1, h], w_s.at[h, 1], w_r.at[h, 1], dev(*left)))

    def w_near(h):
        for ci in (0, 1):
            go(rc(w_ref.at[:, wcol(h, 2 * xs[2] + ci, 1)], wall.at[h, sp], w_s.at[h, 2 + ci], w_r.at[h, 2 + c], dev(xs[2], ci, y)))
            go(rc(w_ref.at[:, wcol(h, 2 * xs[1] + ci, 1)], wall.at[h, sp], w_s.at[h, 4 + ci], w_r.at[h, 4 + c], dev(xs[1], ci, y)))

    def w_pass(h):
        for ci in (0, 1):
            cols = pl.ds(ci * HW, HW)
            go(rc(wst.at[0, h, :, cols], wall.at[h, 2 * xs[1] + c, pl.ds(0, khalf)],
                  w_s.at[h, 6 + ci], w_r.at[h, 6 + c], dev(xs[2], ci, y)))
            go(rc(wst.at[1, h, :, cols], wall.at[h, 2 * xs[2] + c, pl.ds(khalf, khalf)],
                  w_s.at[h, 8 + ci], w_r.at[h, 8 + c], dev(xs[1], ci, y)))

    def w_partner(h):
        go(rc(w_ref.at[:, wcol(h, 2 * xs[0] + 1 - c, 1)], wall.at[h, sp], w_s.at[h, 10], w_r.at[h, 10], partner))

    w_far(0)
    w_partner(0)
    w_partner(1)

    def own(src, via, dst):
        a = pltpu.make_async_copy(src, via, loc.at[5])
        a.start()
        a.wait()
        b = pltpu.make_async_copy(via, dst, loc.at[5])
        b.start()
        b.wait()

    own_in.wait()
    own_out = pltpu.make_async_copy(xown, blk(y, xs[0]), loc.at[0])
    own_out.start()
    for h in (0, 1):
        own(w_ref.at[:, wcol(h, sp, 1)], wbuf.at[h], wall.at[h, sp])
    own(seg_ref, sown, segall.at[sp])

    def wait(dst, sem):
        pltpu.make_async_copy(dst, dst, sem).wait()

    def y_send(i):
        go(rc(blk(y, xs[i]), blk(y, xs[i]), y_s.at[0, i], y_r.at[0, i], dev(xs[0], c, ys[2])))
        go(rc(blk(y, xs[i]), blk(y, xs[i]), y_s.at[1, i], y_r.at[1, i], dev(xs[0], c, ys[1])))

    def to_partner(j, i):
        go(rc(blk(ys[j], xs[i]), blk(ys[j], xs[i]), p_s.at[j, i], p_r.at[j, i], partner))

    wait(blk(y, xs[1]), xs_r.at[0])
    go(rc(blk(y, xs[1]).at[pl.ds(0, half)], blk(y, xs[1]).at[pl.ds(0, half)], xs_s.at[2], xs_r.at[2], dev(*right)))
    wait(blk(y, xs[2]), xs_r.at[1])
    go(rc(blk(y, xs[2]).at[pl.ds(half, half)], blk(y, xs[2]).at[pl.ds(half, half)], xs_s.at[3], xs_r.at[3], dev(*left)))
    w_near(0)
    for i in (1, 2):
        y_send(i)
        to_partner(0, i)

    def y_pass(i):
        wait(blk(ys[1], xs[i]), y_r.at[0, i])
        if i in (0, 3):
            go(rc(blk(ys[1], xs[i]), blk(ys[1], xs[i]), y_s.at[2, i], y_r.at[2, i], dev(xs[0], c, ys[2])))
        to_partner(1, i)
        wait(blk(ys[2], xs[i]), y_r.at[1, i])
        if i in (1, 2):
            go(rc(blk(ys[2], xs[i]), blk(ys[2], xs[i]), y_s.at[2, i], y_r.at[2, i], dev(xs[0], c, ys[1])))
        to_partner(2, i)

    y_pass(0)
    wait(wst.at[0, 0], w_r.at[0, 0])
    wait(wst.at[1, 0], w_r.at[0, 1])
    w_pass(0)
    w_far(1)
    w_near(1)
    wait(blk(y, xs[3]).at[pl.ds(0, half)], xs_r.at[2])
    wait(blk(y, xs[3]).at[pl.ds(half, half)], xs_r.at[3])
    y_send(3)
    to_partner(0, 3)

    acc[...] = jnp.zeros_like(acc)
    y_pass(1)
    y_pass(2)
    y_pass(3)

    def from_partner(j):
        for i in range(4):
            d = xall.at[ys[j], 2 * xs[i] + 1 - c]
            wait(d, p_r.at[j, i])

    def w_wait_near(h):
        for ci in (0, 1):
            wait(wall.at[h, 2 * xs[1] + ci], w_r.at[h, 2 + ci])
            wait(wall.at[h, 2 * xs[2] + ci], w_r.at[h, 4 + ci])

    def w_wait_far(h):
        for ci in (0, 1):
            wait(wall.at[h, 2 * xs[3] + ci, pl.ds(0, khalf)], w_r.at[h, 6 + ci])
            wait(wall.at[h, 2 * xs[3] + ci, pl.ds(khalf, khalf)], w_r.at[h, 8 + ci])

    def run(h, count, src_of):
        def load(i, slot):
            s = src_of(i)
            k, part = s // 2, s % 2
            cols = pl.ds(pl.multiple_of(part * krows, 128), krows)
            xc = [pltpu.make_async_copy(xall.at[k, r, :, cols], xbuf.at[slot, pl.ds(r * rows, rows)], loc.at[1 + slot])
                  for r in range(nsp)]
            wc = pltpu.make_async_copy(wall.at[h, s], wbuf.at[slot], loc.at[3 + slot])
            return xc, wc

        def start(i, slot):
            xc, wc = load(i, slot)
            for cp in xc:
                cp.start()
            wc.start()

        start(0, 0)

        def step(i, carry):
            slot = lax.rem(i, 2)

            @pl.when(i + 1 < count)
            def _():
                start(i + 1, 1 - slot)

            _, wc = load(i, slot)
            pltpu.make_async_copy(xbuf.at[slot], xbuf.at[slot], loc.at[1 + slot]).wait()
            wc.wait()

            def mm(rb, carry):
                r = pl.ds(pl.multiple_of(rb * ROWS_MM, ROWS_MM), ROWS_MM)
                acc[h, r, :] += jnp.dot(xbuf[slot, r, :], wbuf[slot], preferred_element_type=F32)
                return carry

            lax.fori_loop(0, tokens // ROWS_MM, mm, 0)
            return carry

        lax.fori_loop(0, count, step, 0)

    def cast(h):
        def body(rb, carry):
            r = pl.ds(pl.multiple_of(rb * ROWS_MM, ROWS_MM), ROWS_MM)
            qkv_ref[h, r, :] = acc[h, r, :].astype(BF16)
            return carry
        lax.fori_loop(0, tokens // ROWS_MM, body, 0)

    nx = nsp // 2

    own_out.wait()
    for j in (0, 1, 2):
        from_partner(j)
    wait(wall.at[0, 2 * xs[0] + 1 - c], w_r.at[0, 10])
    w_wait_near(0)
    w_wait_far(0)
    run(0, 6, lambda i: 2 * lax.rem(ys[1] + i // 2, ntp) + i % 2)
    for i in range(4):
        wait(blk(ys[3], xs[i]), y_r.at[2, i])
        to_partner(3, i)
    wait(wst.at[0, 1], w_r.at[1, 0])
    wait(wst.at[1, 1], w_r.at[1, 1])
    w_pass(1)
    from_partner(3)
    run(0, 2, lambda i: 2 * ys[3] + i)
    cast(0)
    wait(wall.at[1, 2 * xs[0] + 1 - c], w_r.at[1, 10])
    run(1, 2, lambda i: 2 * xs[0] + i)
    w_wait_near(1)
    run(1, 4, lambda i: 2 * lax.rem(xs[1] + 2 * (i // 2), nx) + i % 2)
    w_wait_far(1)
    run(1, 2, lambda i: 2 * xs[3] + i)
    cast(1)

    for back in (1, 2, 3):
        for ci in (0, 1):
            wait(segall.at[2 * xs[back] + ci], s_r.at[back, ci])
    wait(segall.at[2 * xs[0] + 1 - c], s_r.at[0, 1 - c])
    for cp in sends:
        cp.wait_send()


def qkv_call(nsp, ntp, x, seg, w):
    rows, kcols = x.shape
    krows, ncols = w.shape
    tokens = rows * nsp
    dma = pltpu.SemaphoreType.DMA
    out_shape = (
        jax.ShapeDtypeStruct((2, tokens, HW), BF16),
        jax.ShapeDtypeStruct((ntp, nsp, rows, kcols), BF16),
        jax.ShapeDtypeStruct((2, nsp, krows, HW), BF16),
        jax.ShapeDtypeStruct((2, 2, krows // 2, 2 * HW), BF16),
        jax.ShapeDtypeStruct((nsp, 1, rows), jnp.int32),
    )
    return pl.pallas_call(
        functools.partial(qkv_kernel, nsp, ntp),
        name="qkv",
        out_shape=out_shape,
        in_specs=[ANY, ANY, ANY],
        out_specs=(VM, ANY, ANY, ANY, ANY),
        scratch_shapes=[
            pltpu.VMEM((2, tokens, HW), F32),
            pltpu.VMEM((2, tokens, krows), BF16),
            pltpu.VMEM((2, krows, HW), BF16),
            pltpu.VMEM((rows, kcols), BF16),
            pltpu.VMEM((1, rows), jnp.int32),
            dma((6,)),
            dma((4,)), dma((4,)),
            dma((3, 4)), dma((3, 4)),
            dma((4, 4)), dma((4, 4)),
            dma((2, 11)), dma((2, 11)),
            dma((7,)), dma((4, 2)),
        ],
        compiler_params=pltpu.CompilerParams(
            collective_id=0, has_side_effects=True, vmem_limit_bytes=56 * 1024 * 1024),
    )(x, seg, w)


def attn_kernel(nb, lo_ref, hi_ref, segc_ref, segr_ref, q_ref, k_ref, v_ref, o_ref, s_ref):
    i = pl.program_id(1)
    lo, hi = lo_ref[i], hi_ref[i]
    bq, bk = q_ref.shape[1], s_ref.shape[2]
    segc = segc_ref[...]
    q = q_ref[0]

    def cols(kb):
        return pl.ds(pl.multiple_of(kb * bk, bk), bk)

    def scores(kb, m):
        s = lax.dot_general(q, k_ref[0, cols(kb), :], (((1,), (1,)), ((), ())), preferred_element_type=F32)
        s = jnp.where(segc == segr_ref[:, cols(kb)], s * SOFTMAX_SCALE, -jnp.inf)
        s_ref[kb] = s
        return jnp.maximum(m, jnp.max(s, axis=-1, keepdims=True))

    m = lax.fori_loop(lo, hi, scores, jnp.full((bq, 1), -jnp.inf, F32))

    def expo(kb, l):
        e = jnp.exp(s_ref[kb] - m)
        s_ref[kb] = e
        return l + jnp.sum(e, axis=-1, keepdims=True)

    l = lax.fori_loop(lo, hi, expo, jnp.zeros((bq, 1), F32))
    inv = 1.0 / l

    def values(kb, o):
        p = (s_ref[kb] * inv).astype(BF16)
        return o + jnp.dot(p, v_ref[0, cols(kb), :], preferred_element_type=F32)

    o = lax.fori_loop(lo, hi, values, jnp.zeros((bq, HEAD_DIM), F32))
    o_ref[0] = o.astype(BF16)


def attention(qkv, seg, bq=256, bk=256):
    heads, tokens, _ = qkv.shape
    nq, nb = tokens // bq, tokens // bk
    first, last = seg[::bq], seg[bq - 1::bq]
    lo = jnp.sum((seg[None, :] < first[:, None]).astype(jnp.int32), axis=1) // bk
    hi = (jnp.sum((seg[None, :] <= last[:, None]).astype(jnp.int32), axis=1) + bk - 1) // bk
    grid_spec = pltpu.PrefetchScalarGridSpec(
        num_scalar_prefetch=2,
        grid=(heads, nq),
        in_specs=[
            pl.BlockSpec((bq, 1), lambda h, i, *_: (i, 0)),
            pl.BlockSpec((1, tokens), lambda h, i, *_: (0, 0)),
            pl.BlockSpec((1, bq, HEAD_DIM), lambda h, i, *_: (h, i, 0)),
            pl.BlockSpec((1, tokens, HEAD_DIM), lambda h, i, *_: (h, 0, 1)),
            pl.BlockSpec((1, tokens, HEAD_DIM), lambda h, i, *_: (h, 0, 2)),
        ],
        out_specs=pl.BlockSpec((1, bq, HEAD_DIM), lambda h, i, *_: (h, i, 0)),
        scratch_shapes=[pltpu.VMEM((nb, bq, bk), F32)],
    )
    return pl.pallas_call(
        functools.partial(attn_kernel, nb),
        name="attention",
        out_shape=jax.ShapeDtypeStruct((heads, tokens, HEAD_DIM), BF16),
        grid_spec=grid_spec,
    )(lo, hi, seg[:, None], seg[None, :], qkv, qkv, qkv)


def solution(mesh):
    nsp, ntp = mesh.shape["sp"], mesh.shape["tp"]

    def device_block(x_block, doc_block, wqkv_block, wout_block):
        rows = x_block.shape[0]
        qkv, _, _, _, segall = qkv_call(nsp, ntp, x_block, doc_block.reshape(1, rows), wqkv_block)
        context = attention(qkv, segall.reshape(nsp * rows))
        context = context.reshape(2, nsp, rows, HEAD_DIM)
        context = lax.all_to_all(context, "sp", 1, 1, tiled=False)
        context = context.transpose(2, 0, 1, 3).reshape(rows, 2 * nsp * HEAD_DIM)
        ctx_rows = lax.all_gather(context, "tp", axis=1, tiled=True)
        wout_cols = lax.all_gather(wout_block, "sp", axis=0, tiled=True)
        y_block = jnp.dot(ctx_rows, wout_cols, preferred_element_type=F32).astype(BF16)
        return lax.all_to_all(y_block, "tp", 0, 1, tiled=True)

    return jax.shard_map(
        device_block,
        mesh=mesh,
        in_specs=(P(("dp", "sp"), "tp"), P(("dp", "sp")), P("sp", "tp"), P("sp", "tp")),
        out_specs=P(("dp", "sp", "tp"), None),
        check_vma=False,
    )
```

time: 872 us -> 529 us (0.61)
  waiting for transfers between devices: 681 us -> 200 us
  Pallas kernels: 0 us -> 256 us
  matrix products: 88.4 us -> 16.3 us
  other arithmetic: 39.2 us -> 1.48 us
    all_gather x3 -> x0, waiting for transfers between devices: 545 us -> none  [the longest x1 436 us: device_block(): wqkv_cols = lax.all_gather(wqkv_block, 'sp', axis=0, tiled=True)]
    pallas_call x0 -> x2, Pallas kernels: none -> 256 us  [the longest x1 205 us: qkv_call(): pl.pallas_call(functools.partial(qkv_kernel, nsp, ntp), name='qkv', out_s...]
    dot_general x4 -> x1, matrix products: 88.4 us -> 16.3 us  [device_block(): jnp.dot(ctx_rows, wout_cols, preferred_element_type=F32).astype(BF16)]
    all_gather x1, waiting for transfers between devices: 86 us -> 156 us  [device_block(): wout_cols = lax.all_gather(wout_block, 'sp', axis=0, tiled=True)]
    sub x1 -> x0, other arithmetic: 38 us -> none  [device_block(): weights = jax.nn.softmax(scores, axis=-1).astype(jnp.bfloat16)]
    all_gather x1 -> x0, blocking collectives: 22.2 us -> none  [device_block(): doc_all = lax.all_gather(doc_block, 'sp', axis=0, tiled=True)]
    all_to_all x0 -> x1, blocking collectives: none -> 19.4 us  [device_block(): context = lax.all_to_all(context, 'sp', 1, 1, tiled=False)]
  transfers between devices with their start and end apart: 5 -> 2, of which waited for: 5 -> 2; matrix products, arithmetic and copies ran while one was open for 8% -> 0% of each run, Pallas kernels for 0% -> 0%
where the time goes in v1:
time: 529 us; the launch traced here: 533 us
  Pallas kernels  256 us (48%)
  waiting for transfers between devices  200 us (38%)
  blocking collectives  39.1 us (7%)
  matrix products  16.3 us (3%)
  between operations  13.5 us (3%)
  local copies, waits for them, and re-layouts  7.17 us (1%)
    pallas_call x1, Pallas kernels, qkv_call(): pl.pallas_call(functools.partial(qkv_kernel, nsp, ntp), name='qkv', out_s...  205 us
    all_gather x1, waiting for transfers between devices, device_block(): wout_cols = lax.all_gather(wout_block, 'sp', axis=0, tiled=True)  156 us
    pallas_call x1, Pallas kernels, attention(): pl.pallas_call(functools.partial(attn_kernel, nb), name='attention', out_...  51.1 us
    all_gather x1, waiting for transfers between devices, device_block(): ctx_rows = lax.all_gather(context, 'tp', axis=1, tiled=True)  42.7 us
    all_to_all x1, blocking collectives, device_block(): return lax.all_to_all(y_block, 'tp', 0, 1, tiled=True)  19.6 us
    all_to_all x1, blocking collectives, device_block(): context = lax.all_to_all(context, 'sp', 1, 1, tiled=False)  19.4 us
    dot_general x1, matrix products, device_block(): jnp.dot(ctx_rows, wout_cols, preferred_element_type=F32).astype(BF16)  16.3 us
  transfers between devices with their start and end apart: 2, of which 2 were waited for; matrix products, arithmetic and copies ran while one was open for 0% of the time, Pallas kernels for 0%

profile of v1, /device:TPU:98, one launch (start us, length us, event | category | flops | bytes accessed | tf_op | source)
XLA Modules:
  0.0 533.0 jit_solution(15321836629494575735)
XLA Ops:
  6.5 0.0 all-gather.3.cloned.1.call-start
  6.6 204.7 %qkv.1 = (bf16[2,2048,384]{2,1,0:T(8,128)(2,1)}, bf16[4,8,256,2048]{3,2,1,0:T(8,128)(2,1)}, bf16[2,8,1024,384]{3,2,1,0:T(8,128)(2,1)}, bf16[2,2,512,768]{3,2,1,0:T(8,128)(2,1)}, s32[8,1,256]{2,1,0:T(1,128)}) custom-call(bf16[256,2048]{1,0:T(8,128)(2,1)} %x_ref.1, s32[1,256]{1,0:T(1,128)} %bitcast.23, bf16[1024,6144]{1,0:T(8,128)(2,1)} %w_ref.1), custom_call_target="tpu_custom_call" | custom-call | tf_op jit(solution)/shard_map/qkv/pallas_call | solution.py:280
  211.3 0.8 slice.6
  212.0 0.8 slice.7
  212.8 2.0 copy.13.segc_ref
  214.9 0.9 convert_reduce_fusion
  215.8 0.6 and_select_fusion
  216.3 51.1 %attention.1 = bf16[2,2048,128]{2,1,0:T(8,128)(2,1)} custom-call(s32[8]{0:T(128)} %get-tuple-element.12.lo_ref, s32[8]{0:T(128)} %get-tuple-element.11.hi_ref, s32[2048,1]{1,0:T(8,128)} %copy.13.segc_ref, s32[1,2048]{1,0:T(1,128)} %bitcast.22, bf16[2,2048,384]{2,1,0:T(8,128)(2,1)} %get-tuple-element.8.q_ref.k_ref.v_ref, ...), custom_call_target="tpu_custom_call" | custom-call | tf_op jit(solution)/shard_map/attention/pallas_call | solution.py:357
  267.4 1.5 copy.14
  268.9 19.4 %all_to_all.24 = bf16[2,8,256,128]{2,3,0,1:T(8,128)(2,1)S(1)} all-to-all(bf16[2,8,256,128]{2,3,0,1:T(8,128)(2,1)S(1)} %copy.14), channel_id=1, replica_groups=mesh['dp'=1,'tp'=4,'sp'=8] {'sp'}, dimensions={1} | all-to-all | bytes 2097152 | tf_op jit(solution)/shard_map/all_to_all | solution.py:373
  288.4 1.0 copy.15
  289.4 0.1 all-gather.3.cloned.1.call-update
  289.5 0.1 all-gather.5.cloned.1.call-start
  289.5 0.7 all-gather.5.cloned.1.call-update
  290.3 42.7 %all-gather.3.cloned.1.call-done = bf16[256,8192]{0,1:T(8,128)(2,1)} async-done(((bf16[256,2048]{0,1:T(8,128)(2,1)}), bf16[256,8192]{0,1:T(8,128)(2,1)}) %all-gather.3.cloned.1.call-update) | async-done | bytes 4194320 | tf_op jit(solution)/shard_map/all_gather | solution.py:375
  333.0 156.2 %all-gather.5.cloned.1.call-done = bf16[8192,2048]{1,0:T(8,128)(2,1)} async-done(((bf16[1024,2048]{1,0:T(8,128)(2,1)}), bf16[8192,2048]{1,0:T(8,128)(2,1)}) %all-gather.5.cloned.1.call-update) | async-done | bytes 33554448 | tf_op jit(solution)/shard_map/all_gather | solution.py:376
  489.2 16.3 %convolution_convert_fusion = bf16[256,2048]{1,0:T(8,128)(2,1)S(1)} fusion(bf16[256,8192]{0,1:T(8,128)(2,1)} %all-gather.3.cloned.1.call-done, bf16[8192,2048]{1,0:T(8,128)(2,1)} %all-gather.5.cloned.1.call-done), kind=kOutput, calls=%fused_computation | convolution fusion | flops 8590458880 | bytes 38797312 | tf_op jit(solution)/shard_map/dot_general | solution.py:377
  505.4 19.6 %all_to_all.25 = bf16[4,64,2048]{2,1,0:T(8,128)(2,1)S(1)} all-to-all(bf16[4,64,2048]{2,1,0:T(8,128)(2,1)S(1)} %bitcast.14), channel_id=1, replica_groups=mesh['dp'=1,'tp'=4,'sp'=8] {'tp'}, dimensions={0} | all-to-all | bytes 2097152 | tf_op jit(solution)/shard_map/all_to_all | solution.py:378
  525.1 1.0 copy.17
Async XLA Ops:
  6.5 326.4 %all-gather.3.cloned.1.call-start = ((), (), s32[]{:S(2)}) async-start(), calls=%async_computation.2 | async-start | bytes 5242880 | tf_op jit(solution)/shard_map/all_gather | solution.py:375
  289.5 199.7 %all-gather.5.cloned.1.call-start = ((), (), s32[]{:S(2)}) async-start(), calls=%async_computation.3 | async-start | bytes 37748736 | tf_op jit(solution)/shard_map/all_gather | solution.py:376
Sparse Core Ops, SparseCore 0:
  289.6 43.3 all-gather.2
  334.6 154.5 all-gather.4

commit v2 on v1

--- a/solution.py
+++ b/solution.py
@@ -186,20 +186,16 @@
             wait(wall.at[h, 2 * xs[3] + ci, pl.ds(khalf, khalf)], w_r.at[h, 8 + ci])
 
     def run(h, count, src_of):
-        def load(i, slot):
+        def w_copy(i, slot):
+            return pltpu.make_async_copy(wall.at[h, src_of(i)], wbuf.at[slot], loc.at[3 + slot])
+
+        def start(i, slot):
             s = src_of(i)
-            k, part = s // 2, s % 2
-            cols = pl.ds(pl.multiple_of(part * krows, 128), krows)
-            xc = [pltpu.make_async_copy(xall.at[k, r, :, cols], xbuf.at[slot, pl.ds(r * rows, rows)], loc.at[1 + slot])
-                  for r in range(nsp)]
-            wc = pltpu.make_async_copy(wall.at[h, s], wbuf.at[slot], loc.at[3 + slot])
-            return xc, wc
-
-        def start(i, slot):
-            xc, wc = load(i, slot)
-            for cp in xc:
-                cp.start()
-            wc.start()
+            cols = pl.ds(pl.multiple_of((s % 2) * krows, 128), krows)
+            for r in range(nsp):
+                pltpu.make_async_copy(
+                    xall.at[s // 2, r, :, cols], xbuf.at[slot, pl.ds(r * rows, rows)], loc.at[1 + slot]).start()
+            w_copy(i, slot).start()
 
         start(0, 0)
 
@@ -210,9 +206,8 @@
             def _():
                 start(i + 1, 1 - slot)
 
-            _, wc = load(i, slot)
-            pltpu.make_async_copy(xbuf.at[slot], xbuf.at[slot], loc.at[1 + slot]).wait()
-            wc.wait()
+            wait(xbuf.at[slot], loc.at[1 + slot])
+            w_copy(i, slot).wait()
 
             def mm(rb, carry):
                 r = pl.ds(pl.multiple_of(rb * ROWS_MM, ROWS_MM), ROWS_MM)
@@ -332,7 +327,7 @@
         return o + jnp.dot(p, v_ref[0, cols(kb), :], preferred_element_type=F32)
 
     o = lax.fori_loop(lo, hi, values, jnp.zeros((bq, HEAD_DIM), F32))
-    o_ref[0] = o.astype(BF16)
+    o_ref[...] = o.astype(BF16)
 
 
 def attention(qkv, seg, bq=256, bk=256):
@@ -351,15 +346,338 @@
             pl.BlockSpec((1, tokens, HEAD_DIM), lambda h, i, *_: (h, 0, 1)),
             pl.BlockSpec((1, tokens, HEAD_DIM), lambda h, i, *_: (h, 0, 2)),
         ],
-        out_specs=pl.BlockSpec((1, bq, HEAD_DIM), lambda h, i, *_: (h, i, 0)),
+        out_specs=pl.BlockSpec((bq, HEAD_DIM), lambda h, i, *_: (i, h)),
         scratch_shapes=[pltpu.VMEM((nb, bq, bk), F32)],
     )
     return pl.pallas_call(
         functools.partial(attn_kernel, nb),
         name="attention",
-        out_shape=jax.ShapeDtypeStruct((heads, tokens, HEAD_DIM), BF16),
+        out_shape=jax.ShapeDtypeStruct((tokens, heads * HEAD_DIM), BF16),
         grid_spec=grid_spec,
     )(lo, hi, seg[:, None], seg[None, :], qkv, qkv, qkv)
+
+
+def out_kernel(nsp, ntp, o_ref, w_ref, y_ref, og, s1, wo, part, far, near, ybuf,
+               loc, w_s, w_r, a_s, a_r, b_s, b_r, g_s, g_r, p_s, p_r, f_s, f_r, n_s, n_r, y_s, y_r):
+    sp, y, c, xs, ys = _place(nsp, ntp)
+    x = xs[0]
+    nx = nsp // 2
+    tokens, width = o_ref.shape
+    quarter = tokens // nx
+    sub = quarter // ntp
+    kw = nx * width
+    ncol = wo.shape[1]
+    nh = ncol // 2
+    out_rows = y_ref.shape[0]
+
+    def dev(xi, ci, yi):
+        return {"sp": 2 * xi + ci, "tp": yi}
+
+    def rc(src, dst, ss, rs, to):
+        return pltpu.make_async_remote_copy(
+            src_ref=src, dst_ref=dst, send_sem=ss, recv_sem=rs, device_id=to, device_id_type=MESH)
+
+    def wait(dst, sem):
+        pltpu.make_async_copy(dst, dst, sem).wait()
+
+    def wo_rows(j, hc):
+        return pl.ds(pl.multiple_of((j % 2) * kw + (j // 2) * width + hc * HEAD_DIM, 128), HEAD_DIM)
+
+    def w_cols(half):
+        return pl.ds(pl.multiple_of(half * ncol, 128), ncol)
+
+    for j in range(nsp):
+        pltpu.make_async_copy(w_ref.at[pl.ds(j * HEAD_DIM, HEAD_DIM), w_cols(c)], wo.at[wo_rows(j, c)], loc.at[0]).start()
+
+    barrier = pltpu.get_barrier_semaphore()
+    greet = [dev(xs[i], c, y) for i in (1, 2, 3)]
+    greet += [dev(x, ci, ys[i]) for i in (1, 2, 3) for ci in (0, 1)]
+    greet.append(dev(x, 1 - c, y))
+    for d in greet:
+        pl.semaphore_signal(barrier, inc=1, device_id=d, device_id_type=MESH)
+    pl.semaphore_wait(barrier, len(greet))
+
+    sends = []
+
+    def go(cp):
+        cp.start()
+        sends.append(cp)
+
+    partner = dev(x, 1 - c, y)
+
+    def quarter_of(q, g):
+        return lax.rem(g + (2, 1, nx - 1, 0)[q], nx)
+
+    def o_rows(q, r):
+        return o_ref.at[pl.ds(pl.multiple_of(quarter_of(q, y) * quarter + r * sub, sub), sub)]
+
+    def r_rows(r):
+        return pl.ds(pl.multiple_of(r * sub, sub), sub)
+
+    def cell(q, r, xi):
+        return og.at[q, r_rows(r), pl.ds(pl.multiple_of(c * kw + xi * width, 128), width)]
+
+    diagonal = x == y
+
+    def stage1(q):
+        for i in (1, 2, 3):
+            r = ys[i]
+
+            @pl.when(diagonal)
+            def _():
+                rc(o_rows(q, r), cell(q, r, x), a_s.at[q, i], a_r.at[q, y], dev(x, c, r)).start()
+
+            @pl.when(jnp.logical_not(diagonal))
+            def _():
+                rc(o_rows(q, r), s1.at[q, y], a_s.at[q, i], a_r.at[q, y], dev(x, c, r)).start()
+
+        @pl.when(diagonal)
+        def _():
+            pltpu.make_async_copy(o_rows(q, y), cell(q, y, x), loc.at[1 + q]).start()
+
+    def stage2(q):
+        @pl.when(jnp.logical_not(diagonal))
+        def _():
+            rc(o_rows(q, y), cell(q, y, x), b_s.at[q, 0], b_r.at[q, x], dev(y, c, y)).start()
+
+        for i in (1, 2, 3):
+            g = ys[i]
+            wait(s1.at[q, g], a_r.at[q, g])
+
+            @pl.when(g != x)
+            def _():
+                rc(s1.at[q, g], cell(q, y, x), b_s.at[q, i], b_r.at[q, x], dev(g, c, y)).start()
+
+    def block(q, r, core):
+        return og.at[q, r_rows(r), pl.ds(pl.multiple_of(core * kw, 128), kw)]
+
+    def stage3(q):
+        for i in (1, 2, 3):
+            wait(cell(q, y, xs[i]), b_r.at[q, xs[i]])
+
+        @pl.when(diagonal)
+        def _():
+            wait(cell(q, y, x), loc.at[1 + q])
+
+        b = block(q, y, c)
+        go(rc(b, b, p_s.at[q, 0], p_r.at[q, 0], partner))
+        go(rc(b, b, g_s.at[q, 0], g_r.at[q, 0], dev(x, c, ys[2])))
+        go(rc(b, b, g_s.at[q, 1], g_r.at[q, 1], dev(x, c, ys[1])))
+
+    hs = sub // 2
+
+    def pass_on(q):
+        d, u = block(q, ys[1], c), block(q, ys[2], c)
+        top, bottom = pl.ds(0, hs), pl.ds(hs, hs)
+        wait(d, g_r.at[q, 0])
+        go(rc(d.at[top], d.at[top], g_s.at[q, 2], g_r.at[q, 2], dev(x, c, ys[2])))
+        go(rc(d, d, p_s.at[q, 1], p_r.at[q, 1], partner))
+        wait(u, g_r.at[q, 1])
+        go(rc(u.at[bottom], u.at[bottom], g_s.at[q, 3], g_r.at[q, 3], dev(x, c, ys[1])))
+        go(rc(u, u, p_s.at[q, 2], p_r.at[q, 2], partner))
+
+    def far_block(q):
+        b = block(q, ys[3], c)
+        wait(b.at[pl.ds(0, hs)], g_r.at[q, 2])
+        wait(b.at[pl.ds(hs, hs)], g_r.at[q, 3])
+        go(rc(b, b, p_s.at[q, 3], p_r.at[q, 3], partner))
+
+    def from_partner(q, i):
+        wait(block(q, ys[i], 1 - c), p_r.at[q, i])
+
+    nt = 256
+
+    def mm(q, start, count):
+        rows = pl.ds(start, count)
+
+        def body(n, carry):
+            cols = pl.ds(pl.multiple_of(n * nt, nt), nt)
+            part[q, rows, cols] = jnp.dot(og[q, rows, :], wo[:, cols], preferred_element_type=F32)
+            return carry
+
+        lax.fori_loop(0, ncol // nt, body, 0)
+
+    left, right = dev(xs[1], c, y), dev(xs[2], c, y)
+    cl, cr = pl.ds(0, nh), pl.ds(nh, nh)
+
+    def send_far(i):
+        r = r_rows(ys[i])
+        go(rc(part.at[0, r, cl], far.at[0, r], f_s.at[0, i], f_r.at[0, i], right))
+        go(rc(part.at[0, r, cr], far.at[1, r], f_s.at[1, i], f_r.at[1, i], left))
+
+    def send_near_first(q, i):
+        r = r_rows(ys[i])
+        if q == 1:
+            go(rc(part.at[1, r, cr], near.at[0, r, cr], n_s.at[0, 0, i], n_r.at[0, 0, i], right))
+        else:
+            go(rc(part.at[2, r, cl], near.at[1, r, cl], n_s.at[1, 0, i], n_r.at[1, 0, i], left))
+
+    def send_near_second(i):
+        r = r_rows(ys[i])
+        wait(far.at[0, r], f_r.at[0, i])
+        part[1, r, cl] += far[0, r, :]
+        go(rc(part.at[1, r, cl], near.at[0, r, cl], n_s.at[0, 1, i], n_r.at[0, 1, i], right))
+        wait(far.at[1, r], f_r.at[1, i])
+        part[2, r, cr] += far[1, r, :]
+        go(rc(part.at[2, r, cr], near.at[1, r, cr], n_s.at[1, 1, i], n_r.at[1, 1, i], left))
+
+    stage1(0)
+    for j in range(nsp):
+        go(rc(w_ref.at[pl.ds(j * HEAD_DIM, HEAD_DIM), w_cols(1 - c)], wo.at[wo_rows(j, c)], w_s.at[j], w_r.at[0], partner))
+    stage1(1)
+    stage2(0)
+    stage3(0)
+    stage1(2)
+    stage1(3)
+    stage2(1)
+    half_w = wo.at[pl.ds(0, nsp * HEAD_DIM)]
+    wait(half_w, loc.at[0])
+    wait(half_w, w_r.at[0])
+
+    def start_of(i):
+        return pl.multiple_of(ys[i] * sub, sub)
+
+    from_partner(0, 0)
+    mm(0, start_of(0), sub)
+    send_far(0)
+    pass_on(0)
+    stage3(1)
+    for i in (1, 2):
+        from_partner(0, i)
+        mm(0, start_of(i), sub)
+        send_far(i)
+    stage2(2)
+    far_block(0)
+    from_partner(0, 3)
+    mm(0, start_of(3), sub)
+    send_far(3)
+    pass_on(1)
+    stage3(2)
+    stage2(3)
+    far_block(1)
+    for i in range(4):
+        from_partner(1, i)
+    mm(1, 0, quarter)
+    for i in range(4):
+        send_near_first(1, i)
+    pass_on(2)
+    stage3(3)
+    far_block(2)
+    for i in range(4):
+        from_partner(2, i)
+    mm(2, 0, quarter)
+    for i in range(4):
+        send_near_first(2, i)
+    for i in range(3):
+        send_near_second(i)
+    pass_on(3)
+    far_block(3)
+    send_near_second(3)
+    for i in range(4):
+        from_partner(3, i)
+    mm(3, 0, quarter)
+
+    ocols = pl.ds(pl.multiple_of((2 * y + c) * ncol, 128), ncol)
+    per = sub // out_rows
+
+    def owner(i, u):
+        b = ys[i] * per + u
+        return b // ntp, lax.rem(b, ntp)
+
+    def ysrc(i, u):
+        return ybuf.at[pl.ds(pl.multiple_of((ys[i] * per + u) * out_rows, out_rows), out_rows)]
+
+    def to_owner(i, u):
+        ci, yi = owner(i, u)
+        mine = jnp.logical_and(ci == c, yi == y)
+        remote = rc(ysrc(i, u), y_ref.at[:, ocols], y_s.at[i, u], y_r.at[y, c], dev(x, ci, yi))
+        local = pltpu.make_async_copy(ysrc(i, u), y_ref.at[:, ocols], y_s.at[i, u])
+        return mine, remote, local
+
+    for i in range(4):
+        r = r_rows(ys[i])
+        wait(near.at[0, r, cr], n_r.at[0, 0, i])
+        wait(near.at[1, r, cl], n_r.at[1, 0, i])
+        wait(near.at[0, r, cl], n_r.at[0, 1, i])
+        wait(near.at[1, r, cr], n_r.at[1, 1, i])
+        ybuf[r, :] = (part[3, r, :] + near[0, r, :] + near[1, r, :]).astype(BF16)
+        for u in range(per):
+            mine, remote, local = to_owner(i, u)
+
+            @pl.when(mine)
+            def _():
+                local.start()
+
+            @pl.when(jnp.logical_not(mine))
+            def _():
+                remote.start()
+
+    for i in range(4):
+        for ci in (0, 1):
+            if i == 0:
+                continue
+            wait(y_ref.at[:, pl.ds(pl.multiple_of((2 * ys[i] + ci) * ncol, 128), ncol)], y_r.at[ys[i], ci])
+    wait(y_ref.at[:, pl.ds(pl.multiple_of((2 * y + 1 - c) * ncol, 128), ncol)], y_r.at[y, 1 - c])
+    for i in range(4):
+        for u in range(per):
+            mine, remote, local = to_owner(i, u)
+
+            @pl.when(mine)
+            def _():
+                local.wait()
+
+            @pl.when(jnp.logical_not(mine))
+            def _():
+                remote.wait_send()
+    for cp in sends:
+        cp.wait_send()
+    for q in range(4):
+        for i in (1, 2, 3):
+            rc(o_rows(q, ys[i]), s1.at[q, y], a_s.at[q, i], a_r.at[q, y], dev(x, c, ys[i])).wait_send()
+
+            @pl.when(ys[i] != x)
+            def _():
+                rc(s1.at[q, ys[i]], cell(q, y, x), b_s.at[q, i], b_r.at[q, x], dev(ys[i], c, y)).wait_send()
+
+        @pl.when(jnp.logical_not(diagonal))
+        def _():
+            rc(o_rows(q, y), cell(q, y, x), b_s.at[q, 0], b_r.at[q, x], dev(y, c, y)).wait_send()
+
+
+def out_call(nsp, ntp, o, w):
+    tokens, width = o.shape
+    krows, wcols = w.shape
+    nx = nsp // 2
+    quarter, ncol = tokens // nx, wcols // 2
+    sub = quarter // ntp
+    dma = pltpu.SemaphoreType.DMA
+    return pl.pallas_call(
+        functools.partial(out_kernel, nsp, ntp),
+        name="out",
+        out_shape=jax.ShapeDtypeStruct((tokens // (nsp * ntp), ntp * wcols), BF16),
+        in_specs=[ANY, ANY],
+        out_specs=ANY,
+        scratch_shapes=[
+            pltpu.VMEM((4, quarter, nsp * width), BF16),
+            pltpu.VMEM((4, ntp, sub, width), BF16),
+            pltpu.VMEM((2 * krows, ncol), BF16),
+            pltpu.VMEM((4, quarter, ncol), F32),
+            pltpu.VMEM((2, quarter, ncol // 2), F32),
+            pltpu.VMEM((2, quarter, ncol), F32),
+            pltpu.VMEM((quarter, ncol), BF16),
+            dma((5,)),
+            dma((nsp,)), dma((1,)),
+            dma((4, 4)), dma((4, 4)),
+            dma((4, 4)), dma((4, 4)),
+            dma((4, 4)), dma((4, 4)),
+            dma((4, 4)), dma((4, 4)),
+            dma((2, 4)), dma((2, 4)),
+            dma((2, 2, 4)), dma((2, 2, 4)),
+            dma((4, 2)), dma((4, 2)),
+        ],
+        compiler_params=pltpu.CompilerParams(
+            collective_id=1, has_side_effects=True, vmem_limit_bytes=60 * 1024 * 1024),
+    )(o, w)
 
 
 def solution(mesh):
@@ -369,13 +687,7 @@
         rows = x_block.shape[0]
         qkv, _, _, _, segall = qkv_call(nsp, ntp, x_block, doc_block.reshape(1, rows), wqkv_block)
         context = attention(qkv, segall.reshape(nsp * rows))
-        context = context.reshape(2, nsp, rows, HEAD_DIM)
-        context = lax.all_to_all(context, "sp", 1, 1, tiled=False)
-        context = context.transpose(2, 0, 1, 3).reshape(rows, 2 * nsp * HEAD_DIM)
-        ctx_rows = lax.all_gather(context, "tp", axis=1, tiled=True)
-        wout_cols = lax.all_gather(wout_block, "sp", axis=0, tiled=True)
-        y_block = jnp.dot(ctx_rows, wout_cols, preferred_element_type=F32).astype(BF16)
-        return lax.all_to_all(y_block, "tp", 0, 1, tiled=True)
+        return out_call(nsp, ntp, context, wout_block)
 
     return jax.shard_map(
         device_block,

time: 529 us -> 368 us (0.70); the launches traced: 533 us -> 364 us
  waiting for transfers between devices: 200 us -> 0 us
  Pallas kernels: 256 us -> 356 us
  blocking collectives: 39.1 us -> 0 us
  matrix products: 16.3 us -> 0 us
  between operations: 13.5 us -> 0.02 us
    all_gather x2 -> x0, waiting for transfers between devices: 199 us -> none  [the longest x1 156 us: device_block(): wout_cols = lax.all_gather(wout_block, 'sp', axis=0, tiled=True)]
    pallas_call x0 -> x1, Pallas kernels: none -> 110 us  [out_call(): pl.pallas_call(functools.partial(out_kernel, nsp, ntp), name='out', out_s...]
    all_to_all x2 -> x0, blocking collectives: 39.1 us -> none  [the longest x1 19.6 us: device_block(): return lax.all_to_all(y_block, 'tp', 0, 1, tiled=True)]
    dot_general x1 -> x0, matrix products: 16.3 us -> none  [device_block(): jnp.dot(ctx_rows, wout_cols, preferred_element_type=F32).astype(BF16)]
    pallas_call x1, Pallas kernels: 51.1 us -> 41.8 us  [attention(): pl.pallas_call(functools.partial(attn_kernel, nb), name='attention', out_...]
  transfers between devices with their start and end apart: 2 -> 0, of which waited for: 2 -> 0; matrix products, arithmetic and copies ran while one was open for 0% -> 0% of each run, Pallas kernels for 0% -> 0%
where the time goes in v2:
time: 368 us; the launch traced here: 364 us
  Pallas kernels  356 us (97%)
  local copies, waits for them, and re-layouts  5.86 us (2%)
    pallas_call x1, Pallas kernels, qkv_call(): pl.pallas_call(functools.partial(qkv_kernel, nsp, ntp), name='qkv', out_s...  205 us
    pallas_call x1, Pallas kernels, out_call(): pl.pallas_call(functools.partial(out_kernel, nsp, ntp), name='out', out_s...  110 us
    pallas_call x1, Pallas kernels, attention(): pl.pallas_call(functools.partial(attn_kernel, nb), name='attention', out_...  41.8 us

profile of v2, /device:TPU:98, one launch (start us, length us, event | category | flops | bytes accessed | tf_op | source)
XLA Modules:
  0.0 363.9 jit_solution(5099751914130970328)
XLA Ops:
  0.0 204.7 %qkv.1 = (bf16[2,2048,384]{2,1,0:T(8,128)(2,1)}, bf16[4,8,256,2048]{3,2,1,0:T(8,128)(2,1)}, bf16[2,8,1024,384]{3,2,1,0:T(8,128)(2,1)}, bf16[2,2,512,768]{3,2,1,0:T(8,128)(2,1)}, s32[8,1,256]{2,1,0:T(1,128)}) custom-call(bf16[256,2048]{1,0:T(8,128)(2,1)} %x_ref.1, s32[1,256]{1,0:T(1,128)} %bitcast.9, bf16[1024,6144]{1,0:T(8,128)(2,1)} %w_ref.2), custom_call_target="tpu_custom_call" | custom-call | tf_op jit(solution)/shard_map/qkv/pallas_call | solution.py:275
  204.7 0.8 slice.7
  205.5 0.8 slice.6
  206.3 0.9 convert_reduce_fusion
  207.2 0.6 and_select_fusion
  207.8 2.0 copy.6.segc_ref
  209.8 41.8 %attention.1.o_ref = bf16[2048,256]{1,0:T(8,128)(2,1)} custom-call(s32[8]{0:T(128)} %get-tuple-element.12.lo_ref, s32[8]{0:T(128)} %get-tuple-element.11.hi_ref, s32[2048,1]{1,0:T(8,128)} %copy.6.segc_ref, s32[1,2048]{1,0:T(1,128)} %bitcast.8, bf16[2,2048,384]{2,1,0:T(8,128)(2,1)} %get-tuple-element.8.q_ref.k_ref.v_ref, ...), custom_call_target="tpu_custom_call" | custom-call | tf_op jit(solution)/shard_map/attention/pallas_call | solution.py:352
  251.6 110.0 %out.1 = bf16[64,8192]{1,0:T(8,128)(2,1)} custom-call(bf16[2048,256]{1,0:T(8,128)(2,1)} %attention.1.o_ref, bf16[1024,2048]{1,0:T(8,128)(2,1)} %w_ref.3), custom_call_target="tpu_custom_call" | custom-call | tf_op jit(solution)/shard_map/out/pallas_call | solution.py:654
  361.6 2.3 copy.8

commit v3 on v2

--- a/solution.py
+++ b/solution.py
@@ -296,73 +296,50 @@
     )(x, seg, w)
 
 
-def attn_kernel(nb, lo_ref, hi_ref, segc_ref, segr_ref, q_ref, k_ref, v_ref, o_ref, s_ref):
-    i = pl.program_id(1)
-    lo, hi = lo_ref[i], hi_ref[i]
-    bq, bk = q_ref.shape[1], s_ref.shape[2]
-    segc = segc_ref[...]
-    q = q_ref[0]
-
-    def cols(kb):
-        return pl.ds(pl.multiple_of(kb * bk, bk), bk)
-
-    def scores(kb, m):
-        s = lax.dot_general(q, k_ref[0, cols(kb), :], (((1,), (1,)), ((), ())), preferred_element_type=F32)
-        s = jnp.where(segc == segr_ref[:, cols(kb)], s * SOFTMAX_SCALE, -jnp.inf)
-        s_ref[kb] = s
-        return jnp.maximum(m, jnp.max(s, axis=-1, keepdims=True))
-
-    m = lax.fori_loop(lo, hi, scores, jnp.full((bq, 1), -jnp.inf, F32))
-
-    def expo(kb, l):
-        e = jnp.exp(s_ref[kb] - m)
-        s_ref[kb] = e
-        return l + jnp.sum(e, axis=-1, keepdims=True)
-
-    l = lax.fori_loop(lo, hi, expo, jnp.zeros((bq, 1), F32))
-    inv = 1.0 / l
-
-    def values(kb, o):
-        p = (s_ref[kb] * inv).astype(BF16)
-        return o + jnp.dot(p, v_ref[0, cols(kb), :], preferred_element_type=F32)
-
-    o = lax.fori_loop(lo, hi, values, jnp.zeros((bq, HEAD_DIM), F32))
-    o_ref[...] = o.astype(BF16)
-
-
-def attention(qkv, seg, bq=256, bk=256):
-    heads, tokens, _ = qkv.shape
-    nq, nb = tokens // bq, tokens // bk
-    first, last = seg[::bq], seg[bq - 1::bq]
-    lo = jnp.sum((seg[None, :] < first[:, None]).astype(jnp.int32), axis=1) // bk
-    hi = (jnp.sum((seg[None, :] <= last[:, None]).astype(jnp.int32), axis=1) + bk - 1) // bk
-    grid_spec = pltpu.PrefetchScalarGridSpec(
-        num_scalar_prefetch=2,
-        grid=(heads, nq),
-        in_specs=[
-            pl.BlockSpec((bq, 1), lambda h, i, *_: (i, 0)),
-            pl.BlockSpec((1, tokens), lambda h, i, *_: (0, 0)),
-            pl.BlockSpec((1, bq, HEAD_DIM), lambda h, i, *_: (h, i, 0)),
-            pl.BlockSpec((1, tokens, HEAD_DIM), lambda h, i, *_: (h, 0, 1)),
-            pl.BlockSpec((1, tokens, HEAD_DIM), lambda h, i, *_: (h, 0, 2)),
-        ],
-        out_specs=pl.BlockSpec((bq, HEAD_DIM), lambda h, i, *_: (i, h)),
-        scratch_shapes=[pltpu.VMEM((nb, bq, bk), F32)],
-    )
-    return pl.pallas_call(
-        functools.partial(attn_kernel, nb),
-        name="attention",
-        out_shape=jax.ShapeDtypeStruct((tokens, heads * HEAD_DIM), BF16),
-        grid_spec=grid_spec,
-    )(lo, hi, seg[:, None], seg[None, :], qkv, qkv, qkv)
-
-
-def out_kernel(nsp, ntp, o_ref, w_ref, y_ref, og, s1, wo, part, far, near, ybuf,
+EXP_SCALE = SOFTMAX_SCALE * 1.4426950408889634
+
+
+def score_rows(q, k_ref, h, ids, seg_ref, s_ref, chunk=512):
+    tokens = k_ref.shape[1]
+    width = seg_ref.shape[2]
+    top = None
+    for n in range(0, tokens, chunk):
+        keys = k_ref[h, n:n + chunk, HEAD_DIM:2 * HEAD_DIM]
+        s = lax.dot_general(q, keys, (((1,), (1,)), ((), ())), preferred_element_type=F32)
+        for g in range(0, chunk, HEAD_DIM):
+            at = n + g
+            key_ids = seg_ref[at // width, :, at % width:at % width + HEAD_DIM]
+            part = jnp.where(ids == key_ids, s[:, g:g + HEAD_DIM], -jnp.inf)
+            s_ref[:, at:at + HEAD_DIM] = part
+            top = part if top is None else jnp.maximum(top, part)
+    return jnp.max(top, axis=-1, keepdims=True)
+
+
+def exp_rows(s_ref, top):
+    total = None
+    for g in range(0, s_ref.shape[1], HEAD_DIM):
+        e = jnp.exp2((s_ref[:, g:g + HEAD_DIM] - top) * EXP_SCALE)
+        s_ref[:, g:g + HEAD_DIM] = e
+        total = e if total is None else total + e
+    return 1.0 / jnp.sum(total, axis=-1, keepdims=True)
+
+
+def value_rows(s_ref, inv, v_ref, h, chunk=512):
+    o = None
+    for n in range(0, s_ref.shape[1], chunk):
+        p = (s_ref[:, n:n + chunk] * inv).astype(BF16)
+        d = jnp.dot(p, v_ref[h, n:n + chunk, 2 * HEAD_DIM:], preferred_element_type=F32)
+        o = d if o is None else o + d
+    return o
+
+
+def out_kernel(nsp, ntp, qkv_ref, seg_ref, w_ref, y_ref, o_ref, sc0, sc1, og, s1, wo, part, far, near, ybuf,
                loc, w_s, w_r, a_s, a_r, b_s, b_r, g_s, g_r, p_s, p_r, f_s, f_r, n_s, n_r, y_s, y_r):
     sp, y, c, xs, ys = _place(nsp, ntp)
     x = xs[0]
     nx = nsp // 2
     tokens, width = o_ref.shape
+    bq = seg_ref.shape[2]
     quarter = tokens // nx
     sub = quarter // ntp
     kw = nx * width
@@ -419,6 +396,21 @@
 
     diagonal = x == y
 
+    def attend(q):
+        def body(n, carry):
+            start = pl.multiple_of(quarter_of(q, y) * quarter + n * bq, bq)
+            rows = pl.ds(start, bq)
+            ids = jnp.broadcast_to(seg_ref[start // bq], (HEAD_DIM, bq)).T
+            top0 = score_rows(qkv_ref[0, rows, :HEAD_DIM], qkv_ref, 0, ids, seg_ref, sc0)
+            top1 = score_rows(qkv_ref[1, rows, :HEAD_DIM], qkv_ref, 1, ids, seg_ref, sc1)
+            inv0 = exp_rows(sc0, top0)
+            o_ref[rows, :HEAD_DIM] = value_rows(sc0, inv0, qkv_ref, 0).astype(BF16)
+            inv1 = exp_rows(sc1, top1)
+            o_ref[rows, HEAD_DIM:] = value_rows(sc1, inv1, qkv_ref, 1).astype(BF16)
+            return carry
+
+        lax.fori_loop(0, quarter // bq, body, 0)
+
     def stage1(q):
         for i in (1, 2, 3):
             r = ys[i]
@@ -433,7 +425,7 @@
 
         @pl.when(diagonal)
         def _():
-            pltpu.make_async_copy(o_rows(q, y), cell(q, y, x), loc.at[1 + q]).start()
+            cell(q, y, x)[...] = o_rows(q, y)[...]
 
     def stage2(q):
         @pl.when(jnp.logical_not(diagonal))
@@ -454,10 +446,6 @@
     def stage3(q):
         for i in (1, 2, 3):
             wait(cell(q, y, xs[i]), b_r.at[q, xs[i]])
-
-        @pl.when(diagonal)
-        def _():
-            wait(cell(q, y, x), loc.at[1 + q])
 
         b = block(q, y, c)
         go(rc(b, b, p_s.at[q, 0], p_r.at[q, 0], partner))
@@ -521,14 +509,16 @@
         part[2, r, cr] += far[1, r, :]
         go(rc(part.at[2, r, cr], near.at[1, r, cr], n_s.at[1, 1, i], n_r.at[1, 1, i], left))
 
-    stage1(0)
     for j in range(nsp):
         go(rc(w_ref.at[pl.ds(j * HEAD_DIM, HEAD_DIM), w_cols(1 - c)], wo.at[wo_rows(j, c)], w_s.at[j], w_r.at[0], partner))
+    attend(0)
+    stage1(0)
+    attend(1)
     stage1(1)
     stage2(0)
+    attend(2)
+    stage1(2)
     stage3(0)
-    stage1(2)
-    stage1(3)
     stage2(1)
     half_w = wo.at[pl.ds(0, nsp * HEAD_DIM)]
     wait(half_w, loc.at[0])
@@ -540,6 +530,8 @@
     from_partner(0, 0)
     mm(0, start_of(0), sub)
     send_far(0)
+    attend(3)
+    stage1(3)
     pass_on(0)
     stage3(1)
     for i in (1, 2):
@@ -644,8 +636,8 @@
             rc(o_rows(q, y), cell(q, y, x), b_s.at[q, 0], b_r.at[q, x], dev(y, c, y)).wait_send()
 
 
-def out_call(nsp, ntp, o, w):
-    tokens, width = o.shape
+def out_call(nsp, ntp, qkv, seg, w):
+    tokens, width = qkv.shape[1], 2 * HEAD_DIM
     krows, wcols = w.shape
     nx = nsp // 2
     quarter, ncol = tokens // nx, wcols // 2
@@ -655,9 +647,12 @@
         functools.partial(out_kernel, nsp, ntp),
         name="out",
         out_shape=jax.ShapeDtypeStruct((tokens // (nsp * ntp), ntp * wcols), BF16),
-        in_specs=[ANY, ANY],
+        in_specs=[VM, VM, ANY],
         out_specs=ANY,
         scratch_shapes=[
+            pltpu.VMEM((tokens, width), BF16),
+            pltpu.VMEM((seg.shape[2], tokens), F32),
+            pltpu.VMEM((seg.shape[2], tokens), F32),
             pltpu.VMEM((4, quarter, nsp * width), BF16),
             pltpu.VMEM((4, ntp, sub, width), BF16),
             pltpu.VMEM((2 * krows, ncol), BF16),
@@ -665,7 +660,7 @@
             pltpu.VMEM((2, quarter, ncol // 2), F32),
             pltpu.VMEM((2, quarter, ncol), F32),
             pltpu.VMEM((quarter, ncol), BF16),
-            dma((5,)),
+            dma((1,)),
             dma((nsp,)), dma((1,)),
             dma((4, 4)), dma((4, 4)),
             dma((4, 4)), dma((4, 4)),
@@ -677,7 +672,7 @@
         ],
         compiler_params=pltpu.CompilerParams(
             collective_id=1, has_side_effects=True, vmem_limit_bytes=60 * 1024 * 1024),
-    )(o, w)
+    )(qkv, seg, w)
 
 
 def solution(mesh):
@@ -686,8 +681,7 @@
     def device_block(x_block, doc_block, wqkv_block, wout_block):
         rows = x_block.shape[0]
         qkv, _, _, _, segall = qkv_call(nsp, ntp, x_block, doc_block.reshape(1, rows), wqkv_block)
-        context = attention(qkv, segall.reshape(nsp * rows))
-        return out_call(nsp, ntp, context, wout_block)
+        return out_call(nsp, ntp, qkv, segall, wout_block)
 
     return jax.shard_map(
         device_block,

time: 368 us -> 326 us (0.89); the launches traced: 364 us -> 326 us
  Pallas kernels: 356 us -> 324 us
    pallas_call x1 -> x0, Pallas kernels: 41.8 us -> none  [attention(): pl.pallas_call(functools.partial(attn_kernel, nb), name='attention', out_...]
    pallas_call x1, Pallas kernels: 110 us -> 119 us  [out_call(): pl.pallas_call(functools.partial(out_kernel, nsp, ntp), name='out', out_s...]
where the time goes in v3:
time: 326 us
  Pallas kernels  324 us (99%)
    pallas_call x1, Pallas kernels, qkv_call(): pl.pallas_call(functools.partial(qkv_kernel, nsp, ntp), name='qkv', out_s...  205 us
    pallas_call x1, Pallas kernels, out_call(): pl.pallas_call(functools.partial(out_kernel, nsp, ntp), name='out', out_s...  119 us

profile of v3, /device:TPU:98, one launch (start us, length us, event | category | flops | bytes accessed | tf_op | source)
XLA Modules:
  0.0 325.8 jit_solution(15552598312016590217)
XLA Ops:
  0.0 204.7 %qkv.1 = (bf16[2,2048,384]{2,1,0:T(8,128)(2,1)}, bf16[4,8,256,2048]{3,2,1,0:T(8,128)(2,1)}, bf16[2,8,1024,384]{3,2,1,0:T(8,128)(2,1)}, bf16[2,2,512,768]{3,2,1,0:T(8,128)(2,1)}, s32[8,1,256]{2,1,0:T(1,128)}) custom-call(bf16[256,2048]{1,0:T(8,128)(2,1)} %x_ref.1, s32[1,256]{1,0:T(1,128)} %bitcast.1, bf16[1024,6144]{1,0:T(8,128)(2,1)} %w_ref.2), custom_call_target="tpu_custom_call" | custom-call | tf_op jit(solution)/shard_map/qkv/pallas_call | solution.py:275
  204.7 118.9 %out.1 = bf16[64,8192]{1,0:T(8,128)(2,1)} custom-call(bf16[2,2048,384]{2,1,0:T(8,128)(2,1)} %get-tuple-element.7.qkv_ref, s32[8,1,256]{2,1,0:T(1,128)} %get-tuple-element.8.seg_ref, bf16[1024,2048]{1,0:T(8,128)(2,1)} %w_ref.3), custom_call_target="tpu_custom_call" | custom-call | tf_op jit(solution)/shard_map/out/pallas_call | solution.py:646
  323.6 2.3 copy.6

commit v4 on v0

v4 whole, which is shorter than its diff:
```python
import functools

import jax
import jax.numpy as jnp
from jax import lax
from jax.experimental import pallas as pl
from jax.experimental.pallas import tpu as pltpu
from jax.sharding import PartitionSpec as P

HEAD_DIM = 128
SOFTMAX_SCALE = HEAD_DIM ** -0.5
MESH = pl.DeviceIdType.MESH
HW = 3 * HEAD_DIM
BF16 = jnp.bfloat16
F32 = jnp.float32
ANY = pl.BlockSpec(memory_space=pl.ANY)
VM = pl.BlockSpec(memory_space=pltpu.VMEM)
ROWS_MM = 1024


def _place(nsp, ntp):
    sp, y = lax.axis_index("sp"), lax.axis_index("tp")
    x, c = sp // 2, sp % 2
    nx = nsp // 2
    xs = [x, lax.rem(x + nx - 1, nx), lax.rem(x + 1, nx), lax.rem(x + 2, nx)]
    ys = [y, lax.rem(y + ntp - 1, ntp), lax.rem(y + 1, ntp), lax.rem(y + 2, ntp)]
    return sp, y, c, xs, ys


EXP_SCALE = SOFTMAX_SCALE * 1.4426950408889634


def score_rows(q, k_ref, h, ids, seg_ref, s_ref, chunk=512):
    tokens = k_ref.shape[0]
    width = seg_ref.shape[2]
    top = None
    for n in range(0, tokens, chunk):
        keys = k_ref[n:n + chunk, h * HW + HEAD_DIM:h * HW + 2 * HEAD_DIM]
        s = lax.dot_general(q, keys, (((1,), (1,)), ((), ())), preferred_element_type=F32)
        for g in range(0, chunk, HEAD_DIM):
            at = n + g
            key_ids = seg_ref[at // width, :, at % width:at % width + HEAD_DIM]
            part = jnp.where(ids == key_ids, s[:, g:g + HEAD_DIM], -jnp.inf)
            s_ref[:, at:at + HEAD_DIM] = part
            top = part if top is None else jnp.maximum(top, part)
    return jnp.max(top, axis=-1, keepdims=True)


def exp_rows(s_ref, top):
    total = None
    for g in range(0, s_ref.shape[1], HEAD_DIM):
        e = jnp.exp2((s_ref[:, g:g + HEAD_DIM] - top) * EXP_SCALE)
        s_ref[:, g:g + HEAD_DIM] = e
        total = e if total is None else total + e
    return 1.0 / jnp.sum(total, axis=-1, keepdims=True)


def value_rows(s_ref, inv, v_ref, h, chunk=512):
    o = None
    for n in range(0, s_ref.shape[1], chunk):
        p = (s_ref[:, n:n + chunk] * inv).astype(BF16)
        d = jnp.dot(p, v_ref[n:n + chunk, h * HW + 2 * HEAD_DIM:(h + 1) * HW], preferred_element_type=F32)
        o = d if o is None else o + d
    return o


def out_part(nsp, ntp, qkv_ref, seg_ref, w_ref, y_ref, o_ref, sc0, sc1, og, s1, wo, part, far, near, ybuf,
             loc, w_s, w_r, a_s, a_r, b_s, b_r, g_s, g_r, p_s, p_r, f_s, f_r, n_s, n_r, y_s, y_r):
    sp, y, c, xs, ys = _place(nsp, ntp)
    x = xs[0]
    nx = nsp // 2
    tokens, width = o_ref.shape
    bq = seg_ref.shape[2]
    quarter = tokens // nx
    sub = quarter // ntp
    kw = nx * width
    ncol = wo.shape[1]
    nh = ncol // 2
    out_rows = y_ref.shape[0]

    def dev(xi, ci, yi):
        return {"sp": 2 * xi + ci, "tp": yi}

    def rc(src, dst, ss, rs, to):
        return pltpu.make_async_remote_copy(
            src_ref=src, dst_ref=dst, send_sem=ss, recv_sem=rs, device_id=to, device_id_type=MESH)

    def wait(dst, sem):
        pltpu.make_async_copy(dst, dst, sem).wait()

    nw = nsp // 2

    def wo_rows(j, core):
        return pl.ds(pl.multiple_of((j % 2) * kw + (core * (nx // 2) + j // 2) * width, 128), width)

    def wo_src(j, half):
        return w_ref.at[pl.ds(j * width, width), w_cols(half)]

    def w_cols(half):
        return pl.ds(pl.multiple_of(half * ncol, 128), ncol)

    for j in range(nw):
        pltpu.make_async_copy(wo_src(j, c), wo.at[wo_rows(j, c)], loc.at[0]).start()

    sends = []

    def go(cp):
        cp.start()
        sends.append(cp)

    partner = dev(x, 1 - c, y)

    def quarter_of(q, g, low):
        if q in (0, 3):
            return lax.rem(g + (2 if q == 0 else 0), nx)
        return lax.rem(g + jnp.where(jnp.logical_xor(low, q == 2), 1, nx - 1), nx)

    def o_rows(q, r):
        return o_ref.at[pl.ds(pl.multiple_of(quarter_of(q, y, r < ntp // 2) * quarter + r * sub, sub), sub)]

    def r_rows(r):
        return pl.ds(pl.multiple_of(r * sub, sub), sub)

    def cell(q, r, xi):
        return og.at[q, r_rows(r), pl.ds(pl.multiple_of(c * kw + xi * width, 128), width)]

    diagonal = x == y

    def attend(q):
        def body(n, carry):
            start = pl.multiple_of(quarter_of(q, y, n * bq < quarter // 2) * quarter + n * bq, bq)
            rows = pl.ds(start, bq)
            ids = jnp.broadcast_to(seg_ref[start // bq], (HEAD_DIM, bq)).T
            top0 = score_rows(qkv_ref[rows, :HEAD_DIM], qkv_ref, 0, ids, seg_ref, sc0)
            top1 = score_rows(qkv_ref[rows, HW:HW + HEAD_DIM], qkv_ref, 1, ids, seg_ref, sc1)
            inv0 = exp_rows(sc0, top0)
            o_ref[rows, :HEAD_DIM] = value_rows(sc0, inv0, qkv_ref, 0).astype(BF16)
            inv1 = exp_rows(sc1, top1)
            o_ref[rows, HEAD_DIM:] = value_rows(sc1, inv1, qkv_ref, 1).astype(BF16)
            return carry

        lax.fori_loop(0, quarter // bq, body, 0)

    def stage1(q):
        for i in (1, 2, 3):
            r = ys[i]

            @pl.when(diagonal)
            def _():
                rc(o_rows(q, r), cell(q, r, x), a_s.at[q, i], a_r.at[q, y], dev(x, c, r)).start()

            @pl.when(jnp.logical_not(diagonal))
            def _():
                rc(o_rows(q, r), s1.at[q, y], a_s.at[q, i], a_r.at[q, y], dev(x, c, r)).start()

        @pl.when(diagonal)
        def _():
            cell(q, y, x)[...] = o_rows(q, y)[...]

    def stage2(q):
        @pl.when(jnp.logical_not(diagonal))
        def _():
            rc(o_rows(q, y), cell(q, y, x), b_s.at[q, 0], b_r.at[q, x], dev(y, c, y)).start()

        for i in (1, 2, 3):
            g = ys[i]
            wait(s1.at[q, g], a_r.at[q, g])

            @pl.when(g != x)
            def _():
                rc(s1.at[q, g], cell(q, y, x), b_s.at[q, i], b_r.at[q, x], dev(g, c, y)).start()

    def block(q, r, core):
        return og.at[q, r_rows(r), pl.ds(pl.multiple_of(core * kw, 128), kw)]

    def stage3(q):
        for i in (1, 2, 3):
            wait(cell(q, y, xs[i]), b_r.at[q, xs[i]])

        b = block(q, y, c)
        go(rc(b, b, p_s.at[q, 0], p_r.at[q, 0], partner))
        go(rc(b, b, g_s.at[q, 0], g_r.at[q, 0], dev(x, c, ys[2])))
        go(rc(b, b, g_s.at[q, 1], g_r.at[q, 1], dev(x, c, ys[1])))

    hs = sub // 2

    def pass_on(q):
        d, u = block(q, ys[1], c), block(q, ys[2], c)
        top, bottom = pl.ds(0, hs), pl.ds(hs, hs)
        wait(d, g_r.at[q, 0])
        go(rc(d.at[top], d.at[top], g_s.at[q, 2], g_r.at[q, 2], dev(x, c, ys[2])))
        go(rc(d, d, p_s.at[q, 1], p_r.at[q, 1], partner))
        wait(u, g_r.at[q, 1])
        go(rc(u.at[bottom], u.at[bottom], g_s.at[q, 3], g_r.at[q, 3], dev(x, c, ys[1])))
        go(rc(u, u, p_s.at[q, 2], p_r.at[q, 2], partner))

    def far_block(q):
        b = block(q, ys[3], c)
        wait(b.at[pl.ds(0, hs)], g_r.at[q, 2])
        wait(b.at[pl.ds(hs, hs)], g_r.at[q, 3])
        go(rc(b, b, p_s.at[q, 3], p_r.at[q, 3], partner))

    def from_partner(q, i):
        wait(block(q, ys[i], 1 - c), p_r.at[q, i])

    nt = 256

    def mm(q, start, count):
        rows = pl.ds(start, count)

        def body(n, carry):
            cols = pl.ds(pl.multiple_of(n * nt, nt), nt)
            part[q, rows, cols] = jnp.dot(og[q, rows, :], wo[:, cols], preferred_element_type=F32)
            return carry

        lax.fori_loop(0, ncol // nt, body, 0)

    left, right = dev(xs[1], c, y), dev(xs[2], c, y)
    cl, cr = pl.ds(0, nh), pl.ds(nh, nh)

    def send_far(i):
        r = r_rows(ys[i])
        go(rc(part.at[0, r, cl], far.at[0, r], f_s.at[0, i], f_r.at[0, i], right))
        go(rc(part.at[0, r, cr], far.at[1, r], f_s.at[1, i], f_r.at[1, i], left))

    def towards(q, i):
        d = jnp.where(jnp.logical_xor(ys[i] < ntp // 2, q == 2), 0, 1)
        return d, dev(jnp.where(d == 0, xs[2], xs[1]), c, y)

    def half_cols(d):
        return pl.ds(pl.multiple_of(d * nh, nh), nh)

    def send_near_first(q, i):
        r = r_rows(ys[i])
        d, to = towards(q, i)
        cols = half_cols(1 - d)
        go(rc(part.at[q, r, cols], near.at[d, r, cols], n_s.at[q - 1, 0, i], n_r.at[d, 0, i], to))

    def send_near_second(q, i):
        r = r_rows(ys[i])
        d, to = towards(q, i)
        cols = half_cols(d)
        wait(far.at[d, r], f_r.at[d, i])
        part[q, r, cols] += far[d, r, :]
        go(rc(part.at[q, r, cols], near.at[d, r, cols], n_s.at[q - 1, 1, i], n_r.at[d, 1, i], to))

    for j in range(nw):
        go(rc(wo_src(j, 1 - c), wo.at[wo_rows(j, c)], w_s.at[j], w_r.at[0], partner))

    def finish():
        attend(0)
        stage1(0)
        attend(1)
        stage1(1)
        stage2(0)
        attend(2)
        stage1(2)
        stage3(0)
        stage2(1)
        half_w = wo.at[pl.ds(0, nw * width)]
        wait(half_w, loc.at[0])
        wait(half_w, w_r.at[0])

        def start_of(i):
            return pl.multiple_of(ys[i] * sub, sub)

        def piece(q, i):
            from_partner(q, i)
            mm(q, start_of(i), sub)
            send_far(i) if q == 0 else send_near_first(q, i)

        piece(0, 0)
        attend(3)
        stage1(3)
        stage3(1)
        pass_on(0)
        piece(1, 0)
        stage2(2)
        piece(0, 1)
        piece(0, 2)
        stage3(2)
        far_block(0)
        piece(0, 3)
        stage2(3)
        piece(2, 0)
        pass_on(1)
        piece(1, 1)
        piece(1, 2)
        stage3(3)
        far_block(1)
        piece(1, 3)
        pass_on(2)
        piece(2, 1)
        piece(2, 2)
        far_block(2)
        piece(2, 3)
        for i in range(3):
            send_near_second(1, i)
            send_near_second(2, i)
        pass_on(3)
        far_block(3)
        send_near_second(1, 3)
        send_near_second(2, 3)
        for i in range(4):
            from_partner(3, i)
        mm(3, 0, quarter)

        ocols = pl.ds(pl.multiple_of((2 * y + c) * ncol, 128), ncol)
        per = sub // out_rows

        def owner(i, u):
            b = ys[i] * per + u
            return b // ntp, lax.rem(b, ntp)

        def ysrc(i, u):
            return ybuf.at[pl.ds(pl.multiple_of((ys[i] * per + u) * out_rows, out_rows), out_rows)]

        def to_owner(i, u):
            ci, yi = owner(i, u)
            mine = jnp.logical_and(ci == c, yi == y)
            remote = rc(ysrc(i, u), y_ref.at[:, ocols], y_s.at[i, u], y_r.at[y, c], dev(x, ci, yi))
            local = pltpu.make_async_copy(ysrc(i, u), y_ref.at[:, ocols], y_s.at[i, u])
            return mine, remote, local

        for i in range(4):
            r = r_rows(ys[i])
            wait(near.at[0, r, cr], n_r.at[0, 0, i])
            wait(near.at[1, r, cl], n_r.at[1, 0, i])
            wait(near.at[0, r, cl], n_r.at[0, 1, i])
            wait(near.at[1, r, cr], n_r.at[1, 1, i])
            ybuf[r, :] = (part[3, r, :] + near[0, r, :] + near[1, r, :]).astype(BF16)
            for u in range(per):
                mine, remote, local = to_owner(i, u)

                @pl.when(mine)
                def _():
                    local.start()

                @pl.when(jnp.logical_not(mine))
                def _():
                    remote.start()

        for i in range(4):
            for ci in (0, 1):
                if i == 0:
                    continue
                wait(y_ref.at[:, pl.ds(pl.multiple_of((2 * ys[i] + ci) * ncol, 128), ncol)], y_r.at[ys[i], ci])
        wait(y_ref.at[:, pl.ds(pl.multiple_of((2 * y + 1 - c) * ncol, 128), ncol)], y_r.at[y, 1 - c])
        for i in range(4):
            for u in range(per):
                mine, remote, local = to_owner(i, u)

                @pl.when(mine)
                def _():
                    local.wait()

                @pl.when(jnp.logical_not(mine))
                def _():
                    remote.wait_send()
        for cp in sends:
            cp.wait_send()
        for q in range(4):
            for i in (1, 2, 3):
                rc(o_rows(q, ys[i]), s1.at[q, y], a_s.at[q, i], a_r.at[q, y], dev(x, c, ys[i])).wait_send()

                @pl.when(ys[i] != x)
                def _():
                    rc(s1.at[q, ys[i]], cell(q, y, x), b_s.at[q, i], b_r.at[q, x], dev(ys[i], c, y)).wait_send()

            @pl.when(jnp.logical_not(diagonal))
            def _():
                rc(o_rows(q, y), cell(q, y, x), b_s.at[q, 0], b_r.at[q, x], dev(y, c, y)).wait_send()

    return finish


def block_kernel(nsp, ntp, x_ref, seg_ref, w_ref, wo_ref, y_ref, xall, wall,
                 acc, xbuf, wbuf, xown, segall, qkv, o_ref, sc0, sc1, og, s1, wo, part, far, near, ybuf,
                 loc, xs_s, xs_r, xy_s, xy_r, xp_s, xp_r, xw_s, xw_r, id_s, id_r, *out_sems):
    sp, y, c, xs, ys = _place(nsp, ntp)
    rows, kcols = x_ref.shape
    krows = w_ref.shape[0]
    half, khalf = rows // 2, krows // 2
    tokens = rows * nsp

    def dev(xi, ci, yi):
        return {"sp": 2 * xi + ci, "tp": yi}

    def rc(src, dst, ss, rs, to):
        return pltpu.make_async_remote_copy(
            src_ref=src, dst_ref=dst, send_sem=ss, recv_sem=rs, device_id=to, device_id_type=MESH)

    own_in = pltpu.make_async_copy(x_ref, xown, loc.at[0])
    own_in.start()

    barrier = pltpu.get_barrier_semaphore()
    greet = []
    for i in (1, 2, 3):
        for ci in (0, 1):
            greet.append(dev(xs[i], ci, y))
    greet.append(dev(xs[0], 1 - c, y))
    greet += [dev(xs[0], ci, ys[i]) for i in (1, 2, 3) for ci in (0, 1)]
    for d in greet:
        pl.semaphore_signal(barrier, inc=1, device_id=d, device_id_type=MESH)
    pl.semaphore_wait(barrier, len(greet))

    def go(cp):
        cp.start()

    partner = dev(xs[0], 1 - c, y)
    left, right = (xs[1], c, y), (xs[2], c, y)

    def blk(yi, xi):
        return xall.at[yi, 2 * xi + c]

    go(rc(x_ref, blk(y, xs[0]), xs_s.at[0], xs_r.at[0], dev(*right)))
    go(rc(x_ref, blk(y, xs[0]), xs_s.at[1], xs_r.at[1], dev(*left)))
    go(rc(x_ref, blk(y, xs[0]), xy_s.at[0, 0], xy_r.at[0, 0], dev(xs[0], c, ys[2])))
    go(rc(x_ref, blk(y, xs[0]), xy_s.at[1, 0], xy_r.at[1, 0], dev(xs[0], c, ys[1])))
    go(rc(x_ref, blk(y, xs[0]), xp_s.at[0, 0], xp_r.at[0, 0], partner))
    n = 0
    for i in range(4):
        for ci in (0, 1):
            if i == 0 and ci == 1:
                continue
            cc = (1 - c) if i == 0 else ci
            back = {0: 0, 1: 2, 2: 1, 3: 3}[i]
            go(rc(seg_ref, segall.at[sp], id_s.at[n], id_r.at[back, c], dev(xs[i], cc, y)))
            n += 1

    def wcol(j, num):
        return pl.ds(pl.multiple_of(j * 2 * HW, 128), num * 2 * HW)

    def wrow(p):
        return pl.ds(pl.multiple_of(p * khalf, khalf), khalf)

    twins = (c, 1 - c)

    def w_send(p, i, n):
        go(rc(w_ref.at[wrow(p), wcol(2 * xs[i] + twins[n], 1)], wall.at[sp, wrow(p)],
              xw_s.at[p, i, n], xw_r.at[p, (0, 2, 1, 3)[i], n], dev(xs[i], twins[n], y)))

    for n in (0, 1):
        w_send(0, 3, n)
    for p in (0, 1):
        w_send(p, 0, 1)

    finish = out_part(nsp, ntp, qkv, segall, wo_ref, y_ref, o_ref, sc0, sc1, og, s1, wo, part, far, near, ybuf, *out_sems)

    own_in.wait()
    own_out = pltpu.make_async_copy(xown, blk(y, xs[0]), loc.at[0])
    own_out.start()
    ids = pltpu.make_async_copy(seg_ref, segall.at[sp], loc.at[5])
    ids.start()

    def wait(dst, sem):
        pltpu.make_async_copy(dst, dst, sem).wait()

    def y_send(i):
        go(rc(blk(y, xs[i]), blk(y, xs[i]), xy_s.at[0, i], xy_r.at[0, i], dev(xs[0], c, ys[2])))
        go(rc(blk(y, xs[i]), blk(y, xs[i]), xy_s.at[1, i], xy_r.at[1, i], dev(xs[0], c, ys[1])))

    def to_partner(j, i):
        go(rc(blk(ys[j], xs[i]), blk(ys[j], xs[i]), xp_s.at[j, i], xp_r.at[j, i], partner))

    wait(blk(y, xs[1]), xs_r.at[0])
    go(rc(blk(y, xs[1]).at[pl.ds(0, half)], blk(y, xs[1]).at[pl.ds(0, half)], xs_s.at[2], xs_r.at[2], dev(*right)))
    wait(blk(y, xs[2]), xs_r.at[1])
    go(rc(blk(y, xs[2]).at[pl.ds(half, half)], blk(y, xs[2]).at[pl.ds(half, half)], xs_s.at[3], xs_r.at[3], dev(*left)))
    for n in (0, 1):
        w_send(0, 1, n)
        w_send(0, 2, n)
    w_send(1, 3, 0)
    for n in (0, 1):
        w_send(1, 1, n)
        w_send(1, 2, n)
    w_send(1, 3, 1)
    for i in (1, 2):
        y_send(i)
        to_partner(0, i)

    def y_pass(i):
        wait(blk(ys[1], xs[i]), xy_r.at[0, i])
        if i in (0, 3):
            go(rc(blk(ys[1], xs[i]), blk(ys[1], xs[i]), xy_s.at[2, i], xy_r.at[2, i], dev(xs[0], c, ys[2])))
        to_partner(1, i)
        wait(blk(ys[2], xs[i]), xy_r.at[1, i])
        if i in (1, 2):
            go(rc(blk(ys[2], xs[i]), blk(ys[2], xs[i]), xy_s.at[2, i], xy_r.at[2, i], dev(xs[0], c, ys[1])))
        to_partner(2, i)

    y_pass(0)
    wait(blk(y, xs[3]).at[pl.ds(0, half)], xs_r.at[2])
    wait(blk(y, xs[3]).at[pl.ds(half, half)], xs_r.at[3])
    y_send(3)
    to_partner(0, 3)

    acc[...] = jnp.zeros_like(acc)
    y_pass(1)
    y_pass(2)

    def from_partner(j):
        for i in range(4):
            wait(xall.at[ys[j], 2 * xs[i] + 1 - c], xp_r.at[j, i])

    def w_wait(p, i, n):
        wait(wall.at[2 * xs[i] + twins[n], wrow(p)], xw_r.at[p, i, n])

    def x_load(p, s, slot):
        cols = pl.ds(pl.multiple_of((s % 2) * krows + p * khalf, khalf), khalf)
        for r in range(nsp):
            pltpu.make_async_copy(
                xall.at[s // 2, r, :, cols], xbuf.at[slot, pl.ds(r * rows, rows)], loc.at[1 + slot]).start()

    def w_load(p, s, slot):
        @pl.when(s == sp)
        def _():
            pltpu.make_async_copy(w_ref.at[wrow(p), wcol(sp, 1)], wbuf.at[slot], loc.at[3 + slot]).start()

        @pl.when(s != sp)
        def _():
            pltpu.make_async_copy(wall.at[s, wrow(p)], wbuf.at[slot], loc.at[3 + slot]).start()

    def mm(slot, last):
        def body(rb, carry):
            r = pl.ds(pl.multiple_of(rb * ROWS_MM, ROWS_MM), ROWS_MM)
            total = acc[r, :] + jnp.dot(xbuf[slot, r, :], wbuf[slot], preferred_element_type=F32)
            if last:
                qkv[r, :] = total.astype(BF16)
            else:
                acc[r, :] = total
            return carry

        lax.fori_loop(0, tokens // ROWS_MM, body, 0)

    def x_ready(j):
        def ready():
            if j == 1:
                y_pass(3)
            if j == 3:
                for i in range(4):
                    wait(blk(ys[3], xs[i]), xy_r.at[2, i])
                    to_partner(3, i)
            from_partner(j)
        return ready

    nothing = lambda: None

    def arrived(p, *which):
        def waits():
            for i, n in which:
                w_wait(p, i, n)
        return waits

    steps = [
        (0, 2 * ys[0], nothing, nothing), (0, 2 * ys[0] + 1, nothing, nothing),
        (0, 2 * ys[1], x_ready(1), nothing), (0, 2 * ys[1] + 1, nothing, nothing),
        (0, 2 * ys[2], x_ready(2), nothing), (0, 2 * ys[2] + 1, nothing, nothing),
        (0, 2 * ys[3], x_ready(3), nothing), (0, 2 * ys[3] + 1, nothing, nothing),
        (1, sp, nothing, nothing), (1, 2 * xs[0] + 1 - c, nothing, arrived(1, (0, 1))),
        (1, 2 * xs[3] + c, nothing, arrived(1, (3, 0))),
        (1, 2 * xs[1] + c, nothing, arrived(1, (1, 0))), (1, 2 * xs[2] + c, nothing, arrived(1, (2, 0))),
        (1, 2 * xs[1] + 1 - c, nothing, arrived(1, (1, 1))), (1, 2 * xs[2] + 1 - c, nothing, arrived(1, (2, 1))),
        (1, 2 * xs[3] + 1 - c, nothing, arrived(1, (3, 1))),
    ]
    own_out.wait()
    from_partner(0)
    x_load(0, steps[0][1], 0)
    arrived(0, (0, 1), (3, 0), (3, 1), (1, 0), (2, 0), (1, 1), (2, 1))()

    def pick(k, values):
        out = values[-1]
        for n in range(len(values) - 2, -1, -1):
            out = jnp.where(k == n, values[n], out)
        return out

    def at_step(k, n, act):
        if act is not nothing:
            pl.when(k == n)(act)

    count = len(steps)

    def step(k, carry):
        slot = lax.rem(k, 2)
        p, s = k // (count // 2), pick(k, [st[1] for st in steps])
        after = jnp.minimum(k + 1, count - 1)
        ahead = (after // (count // 2), pick(after, [st[1] for st in steps]), 1 - slot)
        for n, st in enumerate(steps):
            at_step(k, n, st[3])
        w_load(p, s, slot)
        held = [n - 1 for n, st in enumerate(steps) if st[2] is not nothing]
        late = functools.reduce(jnp.logical_or, [k == n for n in held + [count - 1]])

        @pl.when(jnp.logical_not(late))
        def _():
            x_load(*ahead)

        wait(xbuf.at[slot], loc.at[1 + slot])
        wait(wbuf.at[slot], loc.at[3 + slot])

        @pl.when(k < count - 1)
        def _():
            mm(slot, False)

        @pl.when(k == count - 1)
        def _():
            mm(slot, True)

        for n in held:
            @pl.when(k == n)
            def _():
                steps[n + 1][2]()
                x_load(*ahead)

        return carry

    lax.fori_loop(0, count, step, 0)

    for back in (1, 2, 3):
        for ci in (0, 1):
            wait(segall.at[2 * xs[back] + ci], id_r.at[back, ci])
    wait(segall.at[2 * xs[0] + 1 - c], id_r.at[0, 1 - c])
    ids.wait()

    finish()

    for n in range(4):
        wait(x_ref if n < 2 else x_ref.at[pl.ds(0, half)], xs_s.at[n])
        for j in range(3):
            wait(x_ref, xy_s.at[j, n])
        for j in range(4):
            wait(x_ref, xp_s.at[j, n])
    for n in range(nsp - 1):
        wait(seg_ref, id_s.at[n])
    for p in (0, 1):
        wait(wall.at[0, wrow(0)], xw_s.at[p, 0, 1])
        for i in (1, 2, 3):
            for n in (0, 1):
                wait(wall.at[0, wrow(0)], xw_s.at[p, i, n])


def block_call(nsp, ntp, x, seg, w, w_out):
    rows, kcols = x.shape
    krows, ocols = w.shape[0], w_out.shape[1]
    tokens, width = rows * nsp, 2 * HEAD_DIM
    quarter, ncol = tokens // (nsp // 2), ocols // 2
    sub = quarter // ntp
    dma, vmem = pltpu.SemaphoreType.DMA, pltpu.VMEM
    out_shape = (
        jax.ShapeDtypeStruct((tokens // (nsp * ntp), ntp * ocols), BF16),
        jax.ShapeDtypeStruct((ntp, nsp, rows, kcols), BF16),
        jax.ShapeDtypeStruct((nsp, krows, 2 * HW), BF16),
    )
    return pl.pallas_call(
        functools.partial(block_kernel, nsp, ntp),
        name="block",
        out_shape=out_shape,
        in_specs=[ANY] * 4,
        out_specs=(ANY,) * 3,
        scratch_shapes=[
            vmem((tokens, 2 * HW), F32),
            vmem((2, tokens, krows // 2), BF16),
            vmem((2, krows // 2, 2 * HW), BF16),
            vmem((rows, kcols), BF16),
            vmem((nsp, 1, rows), jnp.int32),
            vmem((tokens, 2 * HW), BF16),
            vmem((tokens, width), BF16),
            vmem((rows, tokens), F32), vmem((rows, tokens), F32),
            vmem((4, quarter, nsp * width), BF16),
            vmem((4, ntp, sub, width), BF16),
            vmem((2 * w_out.shape[0], ncol), BF16),
            vmem((4, quarter, ncol), F32),
            vmem((2, quarter, ncol // 2), F32),
            vmem((2, quarter, ncol), F32),
            vmem((quarter, ncol), BF16),
            dma((6,)),
            dma((4,)), dma((4,)),
            dma((3, 4)), dma((3, 4)),
            dma((4, 4)), dma((4, 4)),
            dma((2, 4, 2)), dma((2, 4, 2)),
            dma((7,)), dma((4, 2)),
            dma((1,)),
            dma((nsp // 2,)), dma((1,)),
            dma((4, 4)), dma((4, 4)),
            dma((4, 4)), dma((4, 4)),
            dma((4, 4)), dma((4, 4)),
            dma((4, 4)), dma((4, 4)),
            dma((2, 4)), dma((2, 4)),
            dma((2, 2, 4)), dma((2, 2, 4)),
            dma((4, 2)), dma((4, 2)),
        ],
        compiler_params=pltpu.CompilerParams(
            collective_id=0, has_side_effects=True, vmem_limit_bytes=62 * 1024 * 1024),
    )(x, seg, w, w_out)[0]


def solution(mesh):
    nsp, ntp = mesh.shape["sp"], mesh.shape["tp"]

    def device_block(x_block, doc_block, wqkv_block, wout_block):
        return block_call(nsp, ntp, x_block, doc_block.reshape(1, -1), wqkv_block, wout_block)

    return jax.shard_map(
        device_block,
        mesh=mesh,
        in_specs=(P(("dp", "sp"), "tp"), P(("dp", "sp")), P("sp", "tp"), P("sp", "tp")),
        out_specs=P(("dp", "sp", "tp"), None),
        check_vma=False,
    )
```

time: 872 us -> 298 us (0.34)
  waiting for transfers between devices: 681 us -> 0 us
  Pallas kernels: 0 us -> 293 us
  matrix products: 88.4 us -> 0 us
  blocking collectives: 40.3 us -> 0 us
  other arithmetic: 39.2 us -> 0 us
  between operations: 13.2 us -> 0.01 us
    all_gather x5 -> x0, waiting for transfers between devices: 679 us -> none  [the longest x1 436 us: device_block(): wqkv_cols = lax.all_gather(wqkv_block, 'sp', axis=0, tiled=True)]
    pallas_call x0 -> x1, Pallas kernels: none -> 293 us  [block_call(): pl.pallas_call(functools.partial(block_kernel, nsp, ntp), name='block', o...]
    dot_general x4 -> x0, matrix products: 88.4 us -> none  [the longest x1 39.6 us: device_block(): jnp.dot(x_rows, wqkv_cols, preferred_element_type=jnp.float32)]
    sub x1 -> x0, other arithmetic: 38 us -> none  [device_block(): weights = jax.nn.softmax(scores, axis=-1).astype(jnp.bfloat16)]
    all_gather x1 -> x0, blocking collectives: 22.2 us -> none  [device_block(): doc_all = lax.all_gather(doc_block, 'sp', axis=0, tiled=True)]
    all_to_all x1 -> x0, blocking collectives: 18.1 us -> none  [device_block(): return lax.all_to_all(y_block, 'tp', 0, 1, tiled=True)]
  transfers between devices with their start and end apart: 5 -> 0, of which waited for: 5 -> 0; matrix products, arithmetic and copies ran while one was open for 8% -> 0% of each run, Pallas kernels for 0% -> 0%
where the time goes in v4:
time: 298 us; the launch traced here: 295 us
  Pallas kernels  293 us (98%)
    pallas_call x1, Pallas kernels, block_call(): pl.pallas_call(functools.partial(block_kernel, nsp, ntp), name='block', o...  293 us

profile of v4, /device:TPU:98, one launch (start us, length us, event | category | flops | bytes accessed | tf_op | source)
XLA Modules:
  0.0 295.3 jit_solution(6917953979354080915)
XLA Ops:
  0.0 293.0 %block.1 = (bf16[64,8192]{1,0:T(8,128)(2,1)}, bf16[4,8,256,2048]{3,2,1,0:T(8,128)(2,1)}, bf16[8,1024,768]{2,1,0:T(8,128)(2,1)}) custom-call(bf16[256,2048]{1,0:T(8,128)(2,1)} %x_ref.1, s32[1,256]{1,0:T(1,128)} %bitcast.1, bf16[1024,6144]{1,0:T(8,128)(2,1)} %w_ref.1, bf16[1024,2048]{1,0:T(8,128)(2,1)} %wo_ref.1), custom_call_target="tpu_custom_call" | custom-call | tf_op jit(solution)/shard_map/block/pallas_call | solution.py:654
  293.0 2.3 copy.6

commit v5 on v4

--- a/solution.py
+++ b/solution.py
@@ -126,7 +126,7 @@
 
     diagonal = x == y
 
-    def attend(q):
+    def attend(q, first=0, last=None):
         def body(n, carry):
             start = pl.multiple_of(quarter_of(q, y, n * bq < quarter // 2) * quarter + n * bq, bq)
             rows = pl.ds(start, bq)
@@ -139,7 +139,7 @@
             o_ref[rows, HEAD_DIM:] = value_rows(sc1, inv1, qkv_ref, 1).astype(BF16)
             return carry
 
-        lax.fori_loop(0, quarter // bq, body, 0)
+        lax.fori_loop(first, quarter // bq if last is None else last, body, 0)
 
     def stage1(q):
         for i in (1, 2, 3):
@@ -274,32 +274,35 @@
         stage1(3)
         stage3(1)
         pass_on(0)
+        stage2(2)
         piece(1, 0)
-        stage2(2)
         piece(0, 1)
         piece(0, 2)
+        far_block(0)
         stage3(2)
-        far_block(0)
+        stage2(3)
+        pass_on(1)
         piece(0, 3)
-        stage2(3)
-        piece(2, 0)
-        pass_on(1)
         piece(1, 1)
         piece(1, 2)
         stage3(3)
         far_block(1)
+        pass_on(2)
+        piece(2, 0)
         piece(1, 3)
-        pass_on(2)
+        send_near_second(1, 0)
+        send_near_second(1, 1)
+        send_near_second(1, 2)
+        far_block(2)
+        pass_on(3)
         piece(2, 1)
         piece(2, 2)
-        far_block(2)
+        send_near_second(1, 3)
+        far_block(3)
         piece(2, 3)
-        for i in range(3):
-            send_near_second(1, i)
-            send_near_second(2, i)
-        pass_on(3)
-        far_block(3)
-        send_near_second(1, 3)
+        send_near_second(2, 0)
+        send_near_second(2, 1)
+        send_near_second(2, 2)
         send_near_second(2, 3)
         for i in range(4):
             from_partner(3, i)
@@ -374,9 +377,9 @@
     return finish
 
 
-def block_kernel(nsp, ntp, x_ref, seg_ref, w_ref, wo_ref, y_ref, xall, wall,
+def block_kernel(nsp, ntp, x_ref, seg_ref, w_ref, wo_ref, y_ref, xall, wall, wst,
                  acc, xbuf, wbuf, xown, segall, qkv, o_ref, sc0, sc1, og, s1, wo, part, far, near, ybuf,
-                 loc, xs_s, xs_r, xy_s, xy_r, xp_s, xp_r, xw_s, xw_r, id_s, id_r, *out_sems):
+                 loc, xs_s, xs_r, xy_s, xy_r, xp_s, xp_r, xw_s, xw_r, xf_s, xf_r, id_s, id_r, *out_sems):
     sp, y, c, xs, ys = _place(nsp, ntp)
     rows, kcols = x_ref.shape
     krows = w_ref.shape[0]
@@ -403,6 +406,9 @@
     for d in greet:
         pl.semaphore_signal(barrier, inc=1, device_id=d, device_id_type=MESH)
     pl.semaphore_wait(barrier, len(greet))
+
+    def wait(dst, sem):
+        pltpu.make_async_copy(dst, dst, sem).wait()
 
     def go(cp):
         cp.start()
@@ -438,10 +444,32 @@
 
     def w_send(p, i, n):
         go(rc(w_ref.at[wrow(p), wcol(2 * xs[i] + twins[n], 1)], wall.at[sp, wrow(p)],
-              xw_s.at[p, i, n], xw_r.at[p, (0, 2, 1, 3)[i], n], dev(xs[i], twins[n], y)))
-
-    for n in (0, 1):
-        w_send(0, 3, n)
+              xw_s.at[p, i, n], xw_r.at[p, (0, 2, 1)[i], n], dev(xs[i], twins[n], y)))
+
+    kfar = khalf // 2
+
+    def far_rows(p, d):
+        return pl.ds(p * khalf + d * kfar, kfar)
+
+    def w_far(p):
+        for d, to in enumerate((right, left)):
+            go(rc(w_ref.at[far_rows(p, d), wcol(2 * xs[3], 2)], wst.at[d, p], xf_s.at[p, d], xf_r.at[p, d], dev(*to)))
+
+    def w_pass(p):
+        for d in (0, 1):
+            wait(wst.at[d, p], xf_r.at[p, d])
+        for n in (0, 1):
+            cols = pl.ds(pl.multiple_of(twins[n] * 2 * HW, 128), 2 * HW)
+            for d, i in enumerate((2, 1)):
+                go(rc(wst.at[d, p, :, cols], wall.at[2 * xs[3 - i] + c, far_rows(p, d)],
+                      xw_s.at[p, 3 + d, n], xw_r.at[p, 3 + d, n], dev(xs[i], twins[n], y)))
+
+    def w_near(p):
+        for n in (0, 1):
+            w_send(p, 1, n)
+            w_send(p, 2, n)
+
+    w_far(0)
     for p in (0, 1):
         w_send(p, 0, 1)
 
@@ -453,9 +481,6 @@
     ids = pltpu.make_async_copy(seg_ref, segall.at[sp], loc.at[5])
     ids.start()
 
-    def wait(dst, sem):
-        pltpu.make_async_copy(dst, dst, sem).wait()
-
     def y_send(i):
         go(rc(blk(y, xs[i]), blk(y, xs[i]), xy_s.at[0, i], xy_r.at[0, i], dev(xs[0], c, ys[2])))
         go(rc(blk(y, xs[i]), blk(y, xs[i]), xy_s.at[1, i], xy_r.at[1, i], dev(xs[0], c, ys[1])))
@@ -467,14 +492,7 @@
     go(rc(blk(y, xs[1]).at[pl.ds(0, half)], blk(y, xs[1]).at[pl.ds(0, half)], xs_s.at[2], xs_r.at[2], dev(*right)))
     wait(blk(y, xs[2]), xs_r.at[1])
     go(rc(blk(y, xs[2]).at[pl.ds(half, half)], blk(y, xs[2]).at[pl.ds(half, half)], xs_s.at[3], xs_r.at[3], dev(*left)))
-    for n in (0, 1):
-        w_send(0, 1, n)
-        w_send(0, 2, n)
-    w_send(1, 3, 0)
-    for n in (0, 1):
-        w_send(1, 1, n)
-        w_send(1, 2, n)
-    w_send(1, 3, 1)
+    w_near(0)
     for i in (1, 2):
         y_send(i)
         to_partner(0, i)
@@ -490,6 +508,9 @@
         to_partner(2, i)
 
     y_pass(0)
+    w_pass(0)
+    w_far(1)
+    w_near(1)
     wait(blk(y, xs[3]).at[pl.ds(0, half)], xs_r.at[2])
     wait(blk(y, xs[3]).at[pl.ds(half, half)], xs_r.at[3])
     y_send(3)
@@ -504,7 +525,11 @@
             wait(xall.at[ys[j], 2 * xs[i] + 1 - c], xp_r.at[j, i])
 
     def w_wait(p, i, n):
-        wait(wall.at[2 * xs[i] + twins[n], wrow(p)], xw_r.at[p, i, n])
+        if i < 3:
+            wait(wall.at[2 * xs[i] + twins[n], wrow(p)], xw_r.at[p, i, n])
+        else:
+            for d in (0, 1):
+                wait(wall.at[2 * xs[3] + twins[n], far_rows(p, d)], xw_r.at[p, 3 + d, n])
 
     def x_load(p, s, slot):
         cols = pl.ds(pl.multiple_of((s % 2) * krows + p * khalf, khalf), khalf)
@@ -556,11 +581,11 @@
         (0, 2 * ys[0], nothing, nothing), (0, 2 * ys[0] + 1, nothing, nothing),
         (0, 2 * ys[1], x_ready(1), nothing), (0, 2 * ys[1] + 1, nothing, nothing),
         (0, 2 * ys[2], x_ready(2), nothing), (0, 2 * ys[2] + 1, nothing, nothing),
-        (0, 2 * ys[3], x_ready(3), nothing), (0, 2 * ys[3] + 1, nothing, nothing),
+        (0, 2 * ys[3], x_ready(3), lambda: w_pass(1)), (0, 2 * ys[3] + 1, nothing, nothing),
         (1, sp, nothing, nothing), (1, 2 * xs[0] + 1 - c, nothing, arrived(1, (0, 1))),
-        (1, 2 * xs[3] + c, nothing, arrived(1, (3, 0))),
         (1, 2 * xs[1] + c, nothing, arrived(1, (1, 0))), (1, 2 * xs[2] + c, nothing, arrived(1, (2, 0))),
         (1, 2 * xs[1] + 1 - c, nothing, arrived(1, (1, 1))), (1, 2 * xs[2] + 1 - c, nothing, arrived(1, (2, 1))),
+        (1, 2 * xs[3] + c, nothing, arrived(1, (3, 0))),
         (1, 2 * xs[3] + 1 - c, nothing, arrived(1, (3, 1))),
     ]
     own_out.wait()
@@ -634,9 +659,13 @@
         wait(seg_ref, id_s.at[n])
     for p in (0, 1):
         wait(wall.at[0, wrow(0)], xw_s.at[p, 0, 1])
-        for i in (1, 2, 3):
-            for n in (0, 1):
+        for n in (0, 1):
+            for i in (1, 2):
                 wait(wall.at[0, wrow(0)], xw_s.at[p, i, n])
+            for d in (0, 1):
+                wait(wall.at[0, far_rows(0, 0)], xw_s.at[p, 3 + d, n])
+                if n == 0:
+                    wait(wst.at[0, 0], xf_s.at[p, d])
 
 
 def block_call(nsp, ntp, x, seg, w, w_out):
@@ -650,13 +679,14 @@
         jax.ShapeDtypeStruct((tokens // (nsp * ntp), ntp * ocols), BF16),
         jax.ShapeDtypeStruct((ntp, nsp, rows, kcols), BF16),
         jax.ShapeDtypeStruct((nsp, krows, 2 * HW), BF16),
+        jax.ShapeDtypeStruct((2, 2, krows // 4, 4 * HW), BF16),
     )
     return pl.pallas_call(
         functools.partial(block_kernel, nsp, ntp),
         name="block",
         out_shape=out_shape,
         in_specs=[ANY] * 4,
-        out_specs=(ANY,) * 3,
+        out_specs=(ANY,) * 4,
         scratch_shapes=[
             vmem((tokens, 2 * HW), F32),
             vmem((2, tokens, krows // 2), BF16),
@@ -677,7 +707,8 @@
             dma((4,)), dma((4,)),
             dma((3, 4)), dma((3, 4)),
             dma((4, 4)), dma((4, 4)),
-            dma((2, 4, 2)), dma((2, 4, 2)),
+            dma((2, 5, 2)), dma((2, 5, 2)),
+            dma((2, 2)), dma((2, 2)),
             dma((7,)), dma((4, 2)),
             dma((1,)),
             dma((nsp // 2,)), dma((1,)),

time: 298 us -> 291 us (0.977)
  Pallas kernels: 293 us -> 288 us
    pallas_call x1, Pallas kernels: 293 us -> 288 us  [block_call(): pl.pallas_call(functools.partial(block_kernel, nsp, ntp), name='block', o...]
where the time goes in v5:
time: 291 us; the launch traced here: 290 us
  Pallas kernels  288 us (99%)
    pallas_call x1, Pallas kernels, block_call(): pl.pallas_call(functools.partial(block_kernel, nsp, ntp), name='block', o...  288 us

profile of v5, /device:TPU:98, one launch (start us, length us, event | category | flops | bytes accessed | tf_op | source)
XLA Modules:
  0.0 290.5 jit_solution(16064059873311577506)
XLA Ops:
  0.0 288.2 %block.1 = (bf16[64,8192]{1,0:T(8,128)(2,1)}, bf16[4,8,256,2048]{3,2,1,0:T(8,128)(2,1)}, bf16[8,1024,768]{2,1,0:T(8,128)(2,1)}, bf16[2,2,256,1536]{3,2,1,0:T(8,128)(2,1)}) custom-call(bf16[256,2048]{1,0:T(8,128)(2,1)} %x_ref.1, s32[1,256]{1,0:T(1,128)} %bitcast.1, bf16[1024,6144]{1,0:T(8,128)(2,1)} %w_ref.1, bf16[1024,2048]{1,0:T(8,128)(2,1)} %wo_ref.1), custom_call_target="tpu_custom_call" | custom-call | tf_op jit(solution)/shard_map/block/pallas_call | solution.py:684
  288.2 2.3 copy.6

commit v6 on v5

--- a/solution.py
+++ b/solution.py
@@ -378,7 +378,7 @@
 
 
 def block_kernel(nsp, ntp, x_ref, seg_ref, w_ref, wo_ref, y_ref, xall, wall, wst,
-                 acc, xbuf, wbuf, xown, segall, qkv, o_ref, sc0, sc1, og, s1, wo, part, far, near, ybuf,
+                 acc, xbuf, wbuf, wlast, xown, segall, qkv, o_ref, sc0, sc1, og, s1, wo, part, far, near, ybuf,
                  loc, xs_s, xs_r, xy_s, xy_r, xp_s, xp_r, xw_s, xw_r, xf_s, xf_r, id_s, id_r, *out_sems):
     sp, y, c, xs, ys = _place(nsp, ntp)
     rows, kcols = x_ref.shape
@@ -461,7 +461,8 @@
         for n in (0, 1):
             cols = pl.ds(pl.multiple_of(twins[n] * 2 * HW, 128), 2 * HW)
             for d, i in enumerate((2, 1)):
-                go(rc(wst.at[d, p, :, cols], wall.at[2 * xs[3 - i] + c, far_rows(p, d)],
+                dst = wlast.at[pl.ds(d * kfar, kfar)] if (p, n) == (1, 1) else wall.at[2 * xs[3 - i] + c, far_rows(p, d)]
+                go(rc(wst.at[d, p, :, cols], dst,
                       xw_s.at[p, 3 + d, n], xw_r.at[p, 3 + d, n], dev(xs[i], twins[n], y)))
 
     def w_near(p):
@@ -529,7 +530,8 @@
             wait(wall.at[2 * xs[i] + twins[n], wrow(p)], xw_r.at[p, i, n])
         else:
             for d in (0, 1):
-                wait(wall.at[2 * xs[3] + twins[n], far_rows(p, d)], xw_r.at[p, 3 + d, n])
+                got = wlast.at[pl.ds(d * kfar, kfar)] if (p, n) == (1, 1) else wall.at[2 * xs[3] + twins[n], far_rows(p, d)]
+                wait(got, xw_r.at[p, 3 + d, n])
 
     def x_load(p, s, slot):
         cols = pl.ds(pl.multiple_of((s % 2) * krows + p * khalf, khalf), khalf)
@@ -549,7 +551,7 @@
     def mm(slot, last):
         def body(rb, carry):
             r = pl.ds(pl.multiple_of(rb * ROWS_MM, ROWS_MM), ROWS_MM)
-            total = acc[r, :] + jnp.dot(xbuf[slot, r, :], wbuf[slot], preferred_element_type=F32)
+            total = acc[r, :] + jnp.dot(xbuf[slot, r, :], wlast[...] if last else wbuf[slot], preferred_element_type=F32)
             if last:
                 qkv[r, :] = total.astype(BF16)
             else:
@@ -612,7 +614,11 @@
         ahead = (after // (count // 2), pick(after, [st[1] for st in steps]), 1 - slot)
         for n, st in enumerate(steps):
             at_step(k, n, st[3])
-        w_load(p, s, slot)
+
+        @pl.when(k < count - 1)
+        def _():
+            w_load(p, s, slot)
+
         held = [n - 1 for n, st in enumerate(steps) if st[2] is not nothing]
         late = functools.reduce(jnp.logical_or, [k == n for n in held + [count - 1]])
 
@@ -621,10 +627,10 @@
             x_load(*ahead)
 
         wait(xbuf.at[slot], loc.at[1 + slot])
-        wait(wbuf.at[slot], loc.at[3 + slot])
 
         @pl.when(k < count - 1)
         def _():
+            wait(wbuf.at[slot], loc.at[3 + slot])
             mm(slot, False)
 
         @pl.when(k == count - 1)
@@ -691,6 +697,7 @@
             vmem((tokens, 2 * HW), F32),
             vmem((2, tokens, krows // 2), BF16),
             vmem((2, krows // 2, 2 * HW), BF16),
+            vmem((krows // 2, 2 * HW), BF16),
             vmem((rows, kcols), BF16),
             vmem((nsp, 1, rows), jnp.int32),
             vmem((tokens, 2 * HW), BF16),
@@ -725,11 +732,24 @@
     )(x, seg, w, w_out)[0]
 
 
+def copy_kernel(src_ref, dst_ref):
+    dst_ref[...] = src_ref[...]
+
+
+def place(y, parts):
+    rows, cols = y.shape
+    block = pl.BlockSpec((rows, cols // parts), lambda i: (0, i))
+    return pl.pallas_call(
+        copy_kernel, name="place", grid=(parts,), in_specs=[block], out_specs=block,
+        out_shape=jax.ShapeDtypeStruct(y.shape, y.dtype))(y)
+
+
 def solution(mesh):
     nsp, ntp = mesh.shape["sp"], mesh.shape["tp"]
 
     def device_block(x_block, doc_block, wqkv_block, wout_block):
-        return block_call(nsp, ntp, x_block, doc_block.reshape(1, -1), wqkv_block, wout_block)
+        y_block = block_call(nsp, ntp, x_block, doc_block.reshape(1, -1), wqkv_block, wout_block)
+        return place(y_block, ntp)
 
     return jax.shard_map(
         device_block,

time: 291 us -> 292 us (level)
    pallas_call x0 -> x1, Pallas kernels: none -> 3.37 us  [place(): pl.pallas_call(copy_kernel, name='place', grid=(parts,), in_specs=[block]...]
where the time goes in v6:
time: 292 us; the launch traced here: 290 us
  Pallas kernels  290 us (99%)
    pallas_call x1, Pallas kernels, block_call(): pl.pallas_call(functools.partial(block_kernel, nsp, ntp), name='block', o...  287 us

profile of v6, /device:TPU:98, one launch (start us, length us, event | category | flops | bytes accessed | tf_op | source)
XLA Modules:
  0.0 290.4 jit_solution(8503948034838929710)
XLA Ops:
  0.0 287.0 %block.1 = (bf16[64,8192]{1,0:T(8,128)(2,1)}, bf16[4,8,256,2048]{3,2,1,0:T(8,128)(2,1)}, bf16[8,1024,768]{2,1,0:T(8,128)(2,1)}, bf16[2,2,256,1536]{3,2,1,0:T(8,128)(2,1)}) custom-call(bf16[256,2048]{1,0:T(8,128)(2,1)} %x_ref.1, s32[1,256]{1,0:T(1,128)} %bitcast.1, bf16[1024,6144]{1,0:T(8,128)(2,1)} %w_ref.1, bf16[1024,2048]{1,0:T(8,128)(2,1)} %wo_ref.1), custom_call_target="tpu_custom_call" | custom-call | tf_op jit(solution)/shard_map/block/pallas_call | solution.py:690
  287.1 3.4 %place.1 = bf16[64,8192]{1,0:T(8,128)(2,1)} custom-call(bf16[64,8192]{1,0:T(8,128)(2,1)} %get-tuple-element.6.src_ref), custom_call_target="tpu_custom_call" | custom-call | tf_op jit(solution)/shard_map/place/pallas_call | solution.py:742
